TPU v7x, 32 devices: a whole 2x2x4 slice. The times are simulated.
32 devices in a mesh: sector: 16 (over z, y, x), block: 2 (over core).
Axes of the slice: x: 2, y: 2, z: 4, core: 2. Of those that a mesh axis runs over, the one named last changes fastest.
Arguments:
- adjoint_prev: float32 [5, 16, 128, 128], P(None, 'block', 'sector'), may hold values from -6 to 6
- adjoint_source: float32 [5, 16, 128, 128], P(None, 'block', 'sector'), may hold values from -6 to 6
- face_matrices: bfloat16 [3, 5, 5, 16, 128, 128], P(None, None, None, 'block', 'sector'), may hold values from -2.5 to 2.5
- inverse_blocks: bfloat16 [5, 5, 16, 128, 128], P(None, None, 'block', 'sector')
- sector_offset: int32 [1], replicated, may hold values from 1 to 15
- donor_cells: int32 [128], P('sector'), may hold values from 0 to 7
- donor_weights: float32 [128], P('sector'), may hold values from 0.1 to 0.9
Outputs:
- adjoint: float32 [5, 16, 128, 128], P(None, 'block', 'sector')
- last_update: float32 [5, 16, 128, 128], P(None, 'block', 'sector')
All inputs are finite; a program needn't handle non-finite values.
Results may differ from a plain program's by a relative error of at most 0.0003.
Values sent between devices are 32-bit elements; how exact they have to be, the bound alone decides.
A program may use at most 64 MiB of HBM per device.

v0:
```python
import functools

import jax
import jax.numpy as jnp
from jax import lax
from jax.experimental import pallas as pl
from jax.experimental.pallas import tpu as pltpu
from jax.sharding import PartitionSpec as P

ITERS = 4
MESH = pl.DeviceIdType.MESH


def low_part(sectors):
    return max(d for d in range(1, sectors + 1) if sectors % d == 0 and d * d <= sectors)


def kernel(
    sectors,
    blocks,
    prev_ref,
    source_ref,
    face_ref,
    inverse_ref,
    offset_hbm,
    cells_hbm,
    weights_hbm,
    adjoint_ref,
    update_ref,
    offset_ref,
    cells_ref,
    weights_ref,
    field,
    source,
    face16,
    inverse16,
    face,
    inverse,
    partial,
    edge,
    halo,
    rows,
    forward,
    picked,
    blend,
    face_edge,
    inverse_edge,
    source_edge,
    partial_edge,
    local_sem,
    edge_send,
    edge_recv,
    rim_send,
    rim_recv,
    row_send,
    row_recv,
    forward_send,
    forward_recv,
):
    comps, layers, around, lanes = prev_ref.shape
    sector = lax.axis_index("sector")
    block = lax.axis_index("block")
    first = blocks // 2
    lows = low_part(sectors)
    highs = sectors // lows
    high, low = sector // lows, sector % lows
    after, before = (sector + 1) % sectors, (sector + sectors - 1) % sectors
    is_stator_face = block == first
    is_rotor_face = block == first - 1

    barrier = pltpu.get_barrier_semaphore()

    def greet(to_sector, to_block):
        pl.semaphore_signal(barrier, inc=1, device_id=(to_sector, to_block), device_id_type=MESH)

    greet(after, block)
    greet(before, block)

    @pl.when(block > 0)
    def _():
        greet(sector, block - 1)

    @pl.when(block < blocks - 1)
    def _():
        greet(sector, block + 1)

    @pl.when(is_rotor_face)
    def _():
        for step in range(highs):
            greet(((high + step) % highs) * lows + low, first)

    @pl.when(is_stator_face)
    def _():
        for step in range(highs):
            greet(((high + step) % highs) * lows + low, first - 1)
        for step in range(1, lows):
            greet(high * lows + (low + step) % lows, first)

    into_field = pltpu.make_async_copy(prev_ref, field.at[0, :, pl.ds(1, layers)], local_sem.at[0])
    into_source = pltpu.make_async_copy(source_ref, source, local_sem.at[1])
    into_face = pltpu.make_async_copy(face_ref, face16, local_sem.at[2])
    into_inverse = pltpu.make_async_copy(inverse_ref, inverse16, local_sem.at[3])
    into_offset = pltpu.make_async_copy(offset_hbm, offset_ref, local_sem.at[4])
    into_cells = pltpu.make_async_copy(cells_hbm, cells_ref, local_sem.at[5])
    into_weights = pltpu.make_async_copy(weights_hbm, weights_ref, local_sem.at[6])
    scalars = (into_offset, into_cells, into_weights)
    for copy in (into_field,) + scalars + (into_face, into_inverse, into_source):
        copy.start()

    @pl.when(block == 0)
    def _():
        for k in range(ITERS):
            for n in range(comps):
                field[k, n, 0] = jnp.zeros((around, lanes), jnp.float32)

    @pl.when(block == blocks - 1)
    def _():
        for k in range(ITERS):
            for n in range(comps):
                field[k, n, layers + 1] = jnp.zeros((around, lanes), jnp.float32)

    for copy in scalars:
        copy.wait()
    column = lax.broadcasted_iota(jnp.int32, (around, lanes), 0)
    lane = lax.broadcasted_iota(jnp.int32, (around, lanes), 1)
    donor = jnp.zeros((around, lanes), jnp.int32)
    weight = jnp.zeros((around, lanes), jnp.float32)
    for j in range(around):
        donor = jnp.where(column == j, cells_ref[j], donor)
        weight = jnp.where(column == j, weights_ref[j], weight)
    for k in range(around + 1):
        blend[k] = jnp.where(donor == k, weight, 0.0) + jnp.where(donor + 1 == k, 1.0 - weight, 0.0)
    radial_lower = jnp.where(lane == 0, 0.0, 0.6).astype(jnp.float32)
    radial_upper = jnp.where(lane == lanes - 1, 0.0, 0.4).astype(jnp.float32)

    into_field.wait()
    for n in range(comps):
        edge[0, 0, n] = field[0, n, pl.ds(1, layers), around - 1, :]
        edge[0, 1, n] = field[0, n, pl.ds(1, layers), 0, :]

    def edge_copy(k, side):
        return pltpu.make_async_remote_copy(
            src_ref=edge.at[k, side],
            dst_ref=halo.at[k, side],
            send_sem=edge_send.at[k, side],
            recv_sem=edge_recv.at[k, side],
            device_id=(before if side else after, block),
            device_id_type=MESH,
        )

    def rim_copy(k, side):
        return pltpu.make_async_remote_copy(
            src_ref=field.at[k, :, 1 if side else layers],
            dst_ref=field.at[k, :, layers + 1 if side else 0],
            send_sem=rim_send.at[k, side],
            recv_sem=rim_recv.at[k, side],
            device_id=(sector, block - 1 if side else block + 1),
            device_id_type=MESH,
        )

    def row_copy(k, step):
        to = (high + step) % highs
        return pltpu.make_async_remote_copy(
            src_ref=field.at[k, :, layers],
            dst_ref=rows[k].at[high],
            send_sem=row_send.at[k, step],
            recv_sem=row_recv.at[k, step],
            device_id=(to * lows + low, first),
            device_id_type=MESH,
        )

    def row_arrival(k, step):
        origin = (high + highs - step) % highs
        return pltpu.make_async_remote_copy(
            src_ref=field.at[k, :, layers],
            dst_ref=rows[k].at[origin],
            send_sem=row_send.at[k, step],
            recv_sem=row_recv.at[k, step],
            device_id=(origin * lows + low, first),
            device_id_type=MESH,
        )

    def forward_copy(k, step):
        return pltpu.make_async_remote_copy(
            src_ref=forward.at[k],
            dst_ref=picked[k].at[low],
            send_sem=forward_send.at[k, step],
            recv_sem=forward_recv.at[k, step],
            device_id=(high * lows + (low + step) % lows, first),
            device_id_type=MESH,
        )

    def forward_arrival(k, step):
        origin = (low + lows - step) % lows
        return pltpu.make_async_remote_copy(
            src_ref=forward.at[k],
            dst_ref=picked[k].at[origin],
            send_sem=forward_send.at[k, step],
            recv_sem=forward_recv.at[k, step],
            device_id=(high * lows + origin, first),
            device_id_type=MESH,
        )

    def send_rows(k):
        @pl.when(is_rotor_face)
        def _():
            for step in reversed(range(highs)):
                row_copy(k, step).start()

    def send_rims(k):
        @pl.when(block > 0)
        def _():
            rim_copy(k, 1).start()

        @pl.when((block < blocks - 1) & (block != first - 1))
        def _():
            rim_copy(k, 0).start()

    greetings = 2 + (block > 0).astype(jnp.int32) + (block < blocks - 1).astype(jnp.int32)
    greetings += jnp.where(is_rotor_face, highs, 0) + jnp.where(is_stator_face, highs + lows - 1, 0)
    pl.semaphore_wait(barrier, greetings)

    edge_copy(0, 0).start()
    edge_copy(0, 1).start()
    send_rows(0)
    send_rims(0)

    into_face.wait()
    rims = (around - 1, 0)

    def widen(i, carry):
        for d in range(3):
            for m in range(comps):
                face[d, i, m] = face16[d, i, m].astype(jnp.float32)
                for side in range(2):
                    face_edge[d, side, i, m] = face[d, i, m, :, rims[side], :]
        return carry

    lax.fori_loop(0, comps, widen, 0)
    into_inverse.wait()

    def widen_inverse(i, carry):
        for m in range(comps):
            inverse[i, m] = inverse16[i, m].astype(jnp.float32)
            for side in range(2):
                inverse_edge[side, i, m] = inverse[i, m, :, rims[side], :]
        return carry

    lax.fori_loop(0, comps, widen_inverse, 0)
    into_source.wait()
    for side in range(2):
        for m in range(comps):
            source_edge[side, m] = source[m, :, rims[side], :]

    edge_lane = lax.broadcasted_iota(jnp.int32, (layers, lanes), 1)
    edge_lower = jnp.where(edge_lane == 0, 0.0, 0.6).astype(jnp.float32)
    edge_upper = jnp.where(edge_lane == lanes - 1, 0.0, 0.4).astype(jnp.float32)

    def early_edge(k, side):
        inner, share = (around - 2, 0.6) if side == 0 else (1, 0.4)
        acc = [source_edge[side, m] for m in range(comps)]
        for n in range(comps):
            own = edge[k, side, n]
            mix = edge_lower * pltpu.roll(own, 1, 1) + edge_upper * pltpu.roll(own, lanes - 1, 1)
            beside = share * field[k, n, pl.ds(1, layers), inner, :]
            for m in range(comps):
                acc[m] = acc[m] + face_edge[2, side, n, m] * mix + face_edge[1, side, n, m] * beside
        for m in range(comps):
            partial_edge[side, m] = acc[m]

    def late_edge(k, side):
        share = 0.4 if side == 0 else 0.6
        acc = [partial_edge[side, m] for m in range(comps)]
        for n in range(comps):
            lower = field[k, n, pl.ds(0, layers), rims[side], :]
            upper = field[k, n, pl.ds(2, layers), rims[side], :]
            mix = 0.6 * lower + 0.4 * upper
            beside = share * halo[k, 1 - side, n]
            for m in range(comps):
                acc[m] = acc[m] + face_edge[0, side, n, m] * mix + face_edge[1, side, n, m] * beside
        for m in range(comps):
            fresh = inverse_edge[side, m, 0] * acc[0]
            for n in range(1, comps):
                fresh = fresh + inverse_edge[side, m, n] * acc[n]
            edge[k + 1, side, m] = fresh

    def radial(k, a, acc):
        for n in range(comps):
            here = field[k, n, a + 1]
            mix = radial_lower * pltpu.roll(here, 1, 1) + radial_upper * pltpu.roll(here, lanes - 1, 1)
            acc = [acc[m] + face[2, n, m, a] * mix for m in range(comps)]
        return acc

    def axial(k, a, acc):
        for n in range(comps):
            mix = 0.6 * field[k, n, a] + 0.4 * field[k, n, a + 2]
            acc = [acc[m] + face[0, n, m, a] * mix for m in range(comps)]
        return acc

    def circumferential(k, a, acc):
        for n in range(comps):
            here = field[k, n, a + 1]
            minus = jnp.where(column == 0, halo[k, 0, n, pl.ds(a, 1), :], pltpu.roll(here, 1, 0))
            plus = jnp.where(column == around - 1, halo[k, 1, n, pl.ds(a, 1), :], pltpu.roll(here, around - 1, 0))
            mix = 0.6 * minus + 0.4 * plus
            acc = [acc[m] + face[1, n, m, a] * mix for m in range(comps)]
        return acc

    def early(k, a, rim):
        acc = radial(k, a, [source[m, a] for m in range(comps)])
        if not rim:
            acc = axial(k, a, acc)
        for m in range(comps):
            partial[m, a] = acc[m]

    def middle(k, a):
        acc = circumferential(k, a, [partial[m, a] for m in range(comps)])
        for m in range(comps):
            partial[m, a] = acc[m]

    def finish(k, a):
        store(k, a, axial(k, a, [partial[m, a] for m in range(comps)]))

    def late(k, a, rim):
        acc = circumferential(k, a, [partial[m, a] for m in range(comps)])
        if rim:
            acc = axial(k, a, acc)
        store(k, a, acc)

    def store(k, a, acc):
        for m in range(comps):
            fresh = inverse[m, 0, a] * acc[0]
            for n in range(1, comps):
                fresh = fresh + inverse[m, n, a] * acc[n]
            if k < ITERS - 1:
                field[k + 1, m, a + 1] = fresh
            else:
                adjoint_ref[m, a] = 0.0 - fresh
                update_ref[m, a] = field[k, m, a + 1]

    offset = offset_ref[0]
    offset_high, offset_low = offset // lows, offset % lows

    def pass_rows_on(k):
        for step in range(highs):
            row_arrival(k, step).wait_recv()
        whole_from = (high + 2 * highs - offset_high - (low + offset_low) // lows) % highs
        first_from = (high + 2 * highs + 1 - offset_high - (low + offset_low + lows - 1) // lows) % highs
        for n in range(comps):
            forward[k, n] = rows[k][whole_from, n]
            forward[k, comps, n : n + 1, :] = rows[k][first_from, n, 0:1, :]
        for step in range(1, lows):
            forward_copy(k, step).start()
        for n in range(comps + 1):
            picked[k][low, n] = forward[k, n]

    def face_the_rotor(k):
        for step in range(1, lows):
            forward_arrival(k, step).wait_recv()
        row_of = (low + lows - offset_low) % lows
        next_of = (low + lows - offset_low + 1) % lows
        for n in range(comps):
            total = blend[around] * picked[k][next_of, comps, n : n + 1, :]
            for c in range(around):
                total = total + blend[c] * picked[k][row_of, n, c : c + 1, :]
            field[k, n, 0] = total

    def body_of(step, k, rim):
        def body(a, carry):
            step(k, a, rim)
            return carry

        return body

    for k in range(ITERS):
        last = k == ITERS - 1
        lax.fori_loop(1, layers - 1, body_of(early, k, False), 0)
        early(k, 0, True)
        early(k, layers - 1, True)
        if not last:
            early_edge(k, 0)
            early_edge(k, 1)

        @pl.when(is_stator_face)
        def _():
            pass_rows_on(k)

        edge_copy(k, 0).wait_recv()
        edge_copy(k, 1).wait_recv()
        if last:
            lax.fori_loop(1, layers - 1, body_of(late, k, False), 0)
            middle(k, 0)

        @pl.when(block < blocks - 1)
        def _():
            rim_copy(k, 1).wait_recv()

        @pl.when(is_rotor_face)
        def _():
            late(k, layers - 1, True)

        @pl.when((block > 0) & (block != first))
        def _():
            rim_copy(k, 0).wait_recv()

        if last:

            @pl.when(block != first - 1)
            def _():
                late(k, layers - 1, True)

        @pl.when(is_stator_face)
        def _():
            face_the_rotor(k)

        if last:
            finish(k, 0)
        else:
            for side in range(2):
                late_edge(k, side)
                edge_copy(k + 1, side).start()

            @pl.when(is_rotor_face)
            def _():
                for step in reversed(range(highs)):
                    row_copy(k + 1, step).start()

            late(k, 0, True)

            @pl.when(block > 0)
            def _():
                rim_copy(k + 1, 1).start()

            @pl.when(block != first - 1)
            def _():
                late(k, layers - 1, True)

                @pl.when(block < blocks - 1)
                def _():
                    rim_copy(k + 1, 0).start()

            lax.fori_loop(1, layers - 1, body_of(late, k, False), 0)

    for k in range(ITERS):
        edge_copy(k, 0).wait_send()
        edge_copy(k, 1).wait_send()

        @pl.when(block > 0)
        def _():
            rim_copy(k, 1).wait_send()

        @pl.when((block < blocks - 1) & (block != first - 1))
        def _():
            rim_copy(k, 0).wait_send()

        @pl.when(is_rotor_face)
        def _():
            for step in range(highs):
                row_copy(k, step).wait_send()

        @pl.when(is_stator_face)
        def _():
            for step in range(1, lows):
                forward_copy(k, step).wait_send()


def solution(mesh):
    sectors, blocks = mesh.shape["sector"], mesh.shape["block"]
    lows = low_part(sectors)
    highs = sectors // lows

    def sweeps(prev, source, face, inverse, offset, cells, weights):
        comps, layers, around, lanes = prev.shape
        f32, dma = jnp.float32, pltpu.SemaphoreType.DMA
        plane = (around, lanes)
        hbm = pl.BlockSpec(memory_space=pl.ANY)
        vmem = pl.BlockSpec(memory_space=pltpu.VMEM)
        negative, previous = pl.pallas_call(
            functools.partial(kernel, sectors, blocks),
            out_shape=(pltpu.VMEM(prev.shape, f32),) * 2,
            in_specs=[hbm] * 7,
            out_specs=(vmem, vmem),
            scratch_shapes=[
                pltpu.SMEM(offset.shape, offset.dtype),
                pltpu.SMEM(cells.shape, cells.dtype),
                pltpu.SMEM(weights.shape, weights.dtype),
                pltpu.VMEM((ITERS, comps, layers + 2) + plane, f32),
                pltpu.VMEM(prev.shape, f32),
                pltpu.VMEM(face.shape, face.dtype),
                pltpu.VMEM(inverse.shape, inverse.dtype),
                pltpu.VMEM(face.shape, f32),
                pltpu.VMEM(inverse.shape, f32),
                pltpu.VMEM(prev.shape, f32),
                pltpu.VMEM((ITERS, 2, comps, layers, lanes), f32),
                pltpu.VMEM((ITERS, 2, comps, layers, lanes), f32),
                [pltpu.VMEM((highs, comps) + plane, f32)] * ITERS,
                pltpu.VMEM((ITERS, comps + 1) + plane, f32),
                [pltpu.VMEM((lows, comps + 1) + plane, f32)] * ITERS,
                pltpu.VMEM((around + 1,) + plane, f32),
                pltpu.VMEM((3, 2, comps, comps, layers, lanes), f32),
                pltpu.VMEM((2, comps, comps, layers, lanes), f32),
                pltpu.VMEM((2, comps, layers, lanes), f32),
                pltpu.VMEM((2, comps, layers, lanes), f32),
                dma((7,)),
                dma((ITERS, 2)),
                dma((ITERS, 2)),
                dma((ITERS, 2)),
                dma((ITERS, 2)),
                dma((ITERS, highs)),
                dma((ITERS, highs)),
                dma((ITERS, lows)),
                dma((ITERS, lows)),
            ],
            compiler_params=pltpu.CompilerParams(collective_id=0, has_side_effects=True),
        )(prev, source, face, inverse, offset, cells, weights)
        return 0.0 - negative, 0.0 - negative - previous

    return jax.shard_map(
        sweeps,
        mesh=mesh,
        in_specs=(
            P(None, "block", "sector", None),
            P(None, "block", "sector", None),
            P(None, None, None, "block", "sector", None),
            P(None, None, "block", "sector", None),
            P(),
            P("sector"),
            P("sector"),
        ),
        out_specs=(P(None, "block", "sector", None), P(None, "block", "sector", None)),
        check_vma=False,
    )
```

profile of v0, /device:TPU:1, one launch (start us, length us, event | category | flops | bytes accessed | tf_op | source)
XLA Modules:
  0.0 30.2 jit_solution(10896114468276684625)
XLA Ops:
  1.3 28.1 %shard_map.86 = (f32[5,8,8,128]{3,2,1,0:T(8,128)S(1)}, f32[5,8,8,128]{3,2,1,0:T(8,128)S(1)}) custom-call(f32[5,8,8,128]{3,2,1,0:T(8,128)} %prev_ref.1, f32[5,8,8,128]{3,2,1,0:T(8,128)} %source_ref.1, bf16[3,5,5,8,8,128]{5,4,3,2,1,0:T(8,128)(2,1)} %face_ref.1, bf16[5,5,8,8,128]{4,3,2,1,0:T(8,128)(2,1)} %inverse_ref.1, s32[1]{0:T(128)S(6)} %copy.9.offset_hbm, ...), custom_call_target="tpu_custom_call" | custom-call | tf_op jit(solution)/shard_map/pallas_call | solution.py:478
  29.4 0.7 %fusion = (f32[5,8,8,128]{3,2,1,0:T(8,128)}, f32[5,8,8,128]{3,2,1,0:T(8,128)}) fusion(f32[5,8,8,128]{3,2,1,0:T(8,128)S(1)} %get-tuple-element.5, f32[5,8,8,128]{3,2,1,0:T(8,128)S(1)} %get-tuple-element.4), kind=kLoop, calls=%fused_computation.1 | loop fusion | flops 81920 | bytes 655360 | tf_op jit(solution)/shard_map/sub | solution.py:516
where the time goes:
time: 30.3 us; the launch traced here: 30.2 us
  Pallas kernels  28.1 us (93%)
  between operations  1.29 us (4%)
  other arithmetic  0.75 us (2%)
    pallas_call x1, Pallas kernels, sweeps(): pl.pallas_call(functools.partial(kernel, sectors, blocks), out_shape=(plt...  28.1 us
    sub x1, other arithmetic, sweeps(): return (0.0 - negative, 0.0 - negative - previous)  0.75 us

commit v1 on v0

v1 whole, which is shorter than its diff:
```python
import functools

import jax
import jax.numpy as jnp
from jax import lax
from jax.experimental import pallas as pl
from jax.experimental.pallas import tpu as pltpu
from jax.sharding import PartitionSpec as P

ITERS = 4
LOWER, UPPER = 0.6, 0.4
MESH = pl.DeviceIdType.MESH


def low_part(sectors):
    return min(d for d in range(1, sectors + 1) if sectors % d == 0 and d * d >= sectors)


def kernel(
    sectors,
    blocks,
    layers,
    around,
    prev_ref,
    source_ref,
    face_ref,
    inverse_ref,
    offset_hbm,
    cells_hbm,
    weights_hbm,
    adjoint_ref,
    update_ref,
    offset_ref,
    cells_ref,
    weights_ref,
    field,
    source,
    face16,
    inverse16,
    face,
    inverse,
    radial,
    edge,
    halo,
    part,
    part_in,
    coef,
    coef_in,
    axial,
    rim_in,
    row_out,
    rows,
    forward,
    picked,
    cross_out,
    cross,
    cross_forward,
    cross_picked,
    blend,
    local_sem,
    edge_send,
    edge_recv,
    part_send,
    part_recv,
    coef_send,
    coef_recv,
    rim_send,
    rim_recv,
    row_send,
    row_recv,
    forward_send,
    forward_recv,
    cross_send,
    cross_recv,
    cross_forward_send,
    cross_forward_recv,
):
    comps, _, lanes = prev_ref.shape
    pairs = comps * comps
    sector = lax.axis_index("sector")
    block = lax.axis_index("block")
    first = blocks // 2
    lows = low_part(sectors)
    highs = sectors // lows
    high, low = sector // lows, sector % lows
    after, before = (sector + 1) % sectors, (sector + sectors - 1) % sectors
    is_stator_face = block == first
    is_rotor_face = block == first - 1
    has_lower = (block > 0) & (block != first)
    has_upper = (block < blocks - 1) & (block != first - 1)
    rims = (around - 1, 0)

    barrier = pltpu.get_barrier_semaphore()

    def greet(to_sector, to_block):
        pl.semaphore_signal(barrier, inc=1, device_id=(to_sector, to_block), device_id_type=MESH)

    greet(after, block)
    greet(before, block)

    @pl.when(block > 0)
    def _():
        greet(sector, block - 1)

    @pl.when(block < blocks - 1)
    def _():
        greet(sector, block + 1)

    @pl.when(is_rotor_face)
    def _():
        for step in range(highs):
            greet(((high + step) % highs) * lows + low, first)

    @pl.when(is_stator_face)
    def _():
        for step in range(highs):
            greet(((high + step) % highs) * lows + low, first - 1)
        for step in range(1, lows):
            greet(high * lows + (low + step) % lows, first)

    def plane(a):
        return pl.ds(a * around, around) if isinstance(a, int) else pl.ds(pl.multiple_of(a * around, around), around)

    def column_of(c, start=0):
        return pl.ds(start + c, layers, stride=around)

    def item(n):
        return pl.ds(n * layers, layers)

    into_field = pltpu.make_async_copy(prev_ref, field.at[0, :, pl.ds(around, layers * around)], local_sem.at[0])
    into_source = pltpu.make_async_copy(source_ref, source, local_sem.at[1])
    into_face = pltpu.make_async_copy(face_ref, face16, local_sem.at[2])
    into_inverse = pltpu.make_async_copy(inverse_ref, inverse16, local_sem.at[3])
    into_offset = pltpu.make_async_copy(offset_hbm, offset_ref, local_sem.at[4])
    into_cells = pltpu.make_async_copy(cells_hbm, cells_ref, local_sem.at[5])
    into_weights = pltpu.make_async_copy(weights_hbm, weights_ref, local_sem.at[6])
    scalars = (into_offset, into_cells, into_weights)
    for copy in (into_field,) + scalars + (into_inverse, into_face, into_source):
        copy.start()

    nothing = jnp.zeros((around, lanes), jnp.float32)
    for k in range(ITERS):
        for n in range(comps):
            field[k, n, plane(0)] = nothing
            field[k, n, plane(layers + 1)] = nothing

    for copy in scalars:
        copy.wait()
    column = lax.broadcasted_iota(jnp.int32, (around, lanes), 0)
    lane = lax.broadcasted_iota(jnp.int32, (around, lanes), 1)
    donor = jnp.zeros((around, lanes), jnp.int32)
    weight = jnp.zeros((around, lanes), jnp.float32)
    for j in range(around):
        donor = jnp.where(column == j, cells_ref[j], donor)
        weight = jnp.where(column == j, weights_ref[j], weight)
    for c in range(around + 1):
        blend[plane(c)] = jnp.where(donor == c, weight, 0.0) + jnp.where(donor + 1 == c, 1.0 - weight, 0.0)
    radial_lower = jnp.where(lane == 0, 0.0, LOWER).astype(jnp.float32)
    radial_upper = jnp.where(lane == lanes - 1, 0.0, UPPER).astype(jnp.float32)
    around_lower = jnp.where(column == 0, 0.0, LOWER).astype(jnp.float32)
    around_upper = jnp.where(column == around - 1, 0.0, UPPER).astype(jnp.float32)

    offset = offset_ref[0]
    chosen = []
    for step in range(lows):
        to = high * lows + (low + step) % lows
        base = to + 2 * sectors - offset - 1
        ahead = lax.rem(low + lows - lax.rem(base, lows), lows)
        chosen.append(lax.rem(lax.div(base + ahead, lows), highs))
    slots = [lax.rem(low + 2 * sectors - offset - 1 + j, lows) for j in range(4)]

    into_field.wait()

    def take_edges(k):
        for side in range(2):
            for n in range(comps):
                edge[k // 2, side, item(n)] = field[k, n, column_of(rims[side], around)]

    take_edges(0)

    def remote(src, dst, send, recv, to):
        return pltpu.make_async_remote_copy(
            src_ref=src, dst_ref=dst, send_sem=send, recv_sem=recv, device_id=to, device_id_type=MESH
        )

    def beside(side):
        return (before if side else after, block)

    def edge_copy(k, side):
        i = k // 2
        return remote(edge.at[i, side], halo.at[i, side], edge_send.at[i, side], edge_recv.at[i, side], beside(side))

    def part_copy(k, side):
        i = k // 2
        return remote(part.at[i, side], part_in.at[i, side], part_send.at[i, side], part_recv.at[i, side], beside(side))

    def coef_copy(side):
        return remote(coef.at[side], coef_in.at[side], coef_send.at[side], coef_recv.at[side], beside(side))

    def rim_copy(k, side):
        return remote(
            field.at[k, :, plane(1 if side else layers)],
            rim_in.at[k, side],
            rim_send.at[k, side],
            rim_recv.at[k, side],
            (sector, block - 1 if side else block + 1),
        )

    def row_source(k):
        return row_out.at[k // 2] if k % 2 else field.at[k, :, plane(layers)]

    def row_copy(k, step):
        to = (high + step) % highs
        return remote(row_source(k), rows[k].at[high], row_send.at[k, step], row_recv.at[k, step], (to * lows + low, first))

    def row_arrival(k, step):
        origin = (high + highs - step) % highs
        return remote(row_source(k), rows[k].at[origin], row_send.at[k, step], row_recv.at[k, step], (origin * lows + low, first))

    def cross_copy(step):
        to = (high + step) % highs
        return remote(cross_out, cross.at[high], cross_send.at[step], cross_recv.at[step], (to * lows + low, first))

    def cross_arrival(step):
        origin = (high + highs - step) % highs
        return remote(cross_out, cross.at[origin], cross_send.at[step], cross_recv.at[step], (origin * lows + low, first))

    def forward_copy(k, step):
        to = (high * lows + (low + step) % lows, first)
        return remote(forward.at[k, step], picked[k].at[low], forward_send.at[k, step], forward_recv.at[k, step], to)

    def forward_arrival(k, step):
        origin = (low + lows - step) % lows
        to = (high * lows + origin, first)
        return remote(forward.at[k, step], picked[k].at[origin], forward_send.at[k, step], forward_recv.at[k, step], to)

    def cross_forward_copy(step):
        to = (high * lows + (low + step) % lows, first)
        return remote(
            cross_forward.at[step], cross_picked.at[low], cross_forward_send.at[step], cross_forward_recv.at[step], to
        )

    def cross_forward_arrival(step):
        origin = (low + lows - step) % lows
        to = (high * lows + origin, first)
        return remote(
            cross_forward.at[step], cross_picked.at[origin], cross_forward_send.at[step], cross_forward_recv.at[step], to
        )

    far_first = sorted(range(highs), key=lambda step: -min(step, highs - step))

    def send_rows(k):
        for step in far_first:
            row_copy(k, step).start()

    def send_rims(k):
        @pl.when(block > 0)
        def _():
            rim_copy(k, 1).start()

        @pl.when(has_upper)
        def _():
            rim_copy(k, 0).start()

    greetings = 2 + (block > 0).astype(jnp.int32) + (block < blocks - 1).astype(jnp.int32)
    greetings += jnp.where(is_rotor_face, highs, 0) + jnp.where(is_stator_face, highs + lows - 1, 0)
    pl.semaphore_wait(barrier, greetings)

    edge_copy(0, 0).start()
    edge_copy(0, 1).start()

    @pl.when(is_rotor_face)
    def _():
        send_rows(0)

    send_rims(0)

    into_inverse.wait()

    def widen_inverse(i, carry):
        for m in range(comps):
            inverse[i, m] = inverse16[i, m].astype(jnp.float32).reshape(layers * around, lanes)
        return carry

    lax.fori_loop(0, comps, widen_inverse, 0)
    into_face.wait()

    def widen(i, carry):
        for d in range(3):
            for m in range(comps):
                face[d, i, m] = face16[d, i, m].astype(jnp.float32).reshape(layers * around, lanes)
        return carry

    lax.fori_loop(0, comps, widen, 0)

    def product(direction, where, share, store):
        inv = [[inverse[p, m, where] for m in range(comps)] for p in range(comps)]

        def body(n, carry):
            give = [share * face[direction, n, m, where] for m in range(comps)]
            for p in range(comps):
                total = inv[p][0] * give[0]
                for m in range(1, comps):
                    total = total + inv[p][m] * give[m]
                store(n * comps + p, total)
            return carry

        lax.fori_loop(0, comps, body, 0)

    for side, (a, share) in enumerate(((0, LOWER), (layers - 1, UPPER))):

        def keep(i, value):
            axial[side, pl.ds(pl.multiple_of(i * around, around), around)] = value

        product(0, plane(a), share, keep)
    for side in range(2):

        def keep(i, value):
            coef[side, pl.ds(pl.multiple_of(i * layers, layers), layers)] = value

        product(1, column_of(rims[side]), LOWER if side else UPPER, keep)
        for n in range(comps):
            coef[side, pl.ds(pairs * layers + n * comps, comps)] = axial[
                0, pl.ds(n * comps * around + rims[side], comps, stride=around)
            ]
        mixing = pairs * layers + pairs
        coef[side, pl.ds(mixing, around)] = blend[pl.ds(rims[side], around, stride=around)]
        coef[side, pl.ds(mixing + around, 1)] = blend[pl.ds(around * around + rims[side], 1)]

    into_source.wait()

    def make_radial(k):
        for n in range(comps):
            for a in range(layers):
                here = field[k, n, plane(a + 1)]
                radial[n, plane(a)] = radial_lower * pltpu.roll(here, 1, 1) + radial_upper * pltpu.roll(here, lanes - 1, 1)

    def local_part(k, a):
        acc = [source[m, plane(a)] for m in range(comps)]
        for n in range(comps):
            mix = radial[n, plane(a)]
            acc = [acc[m] + face[2, n, m, plane(a)] * mix for m in range(comps)]
        for n in range(comps):
            here = field[k, n, plane(a + 1)]
            mix = around_lower * pltpu.roll(here, 1, 0) + around_upper * pltpu.roll(here, around - 1, 0)
            acc = [acc[m] + face[1, n, m, plane(a)] * mix for m in range(comps)]
        for n in range(comps):
            mix = LOWER * field[k, n, plane(a)] + UPPER * field[k, n, plane(a + 2)]
            acc = [acc[m] + face[0, n, m, plane(a)] * mix for m in range(comps)]
        for m in range(comps):
            fresh = inverse[m, 0, plane(a)] * acc[0]
            for n in range(1, comps):
                fresh = fresh + inverse[m, n, plane(a)] * acc[n]
            if k < ITERS - 1:
                field[k + 1, m, plane(a + 1)] = fresh
            else:
                adjoint_ref[m, plane(a)] = 0.0 - fresh

    def local_parts(k, start, stop):
        def body(a, carry):
            local_part(k, a)
            return carry

        lax.fori_loop(start, stop, body, 0, unroll=UNROLL)

    def add_column(k, side, m, value):
        if k < ITERS - 1:
            where = column_of(rims[side], around)
            field[k + 1, m, where] = field[k + 1, m, where] + value
        else:
            where = column_of(rims[side])
            adjoint_ref[m, where] = adjoint_ref[m, where] - value

    def add_plane(k, a, m, value):
        if k < ITERS - 1:
            field[k + 1, m, plane(a + 1)] = field[k + 1, m, plane(a + 1)] + value
        else:
            adjoint_ref[m, plane(a)] = adjoint_ref[m, plane(a)] - value

    def halo_of(k, s):
        i = k // 2
        if k % 2 == 0:
            return [halo[i, s, item(n)] for n in range(comps)]
        own = [edge[i, 1 - s, item(n)] for n in range(comps)]
        values = []
        for m in range(comps):
            total = part_in[i, s, item(m)]
            for n in range(comps):
                total = total + coef_in[s, item(n * comps + m)] * own[n]
            values.append(total)
        return values

    def fix_sides(k):
        for side in range(2):
            given = halo_of(k, 1 - side)
            for m in range(comps):
                total = coef[side, item(m)] * given[0]
                for n in range(1, comps):
                    total = total + coef[side, item(n * comps + m)] * given[n]
                add_column(k, side, m, total)

    def fix_layer(k, upper, given):
        a = layers - 1 if upper else 0
        for m in range(comps):
            total = axial[upper, plane(m)] * given[0]
            for n in range(1, comps):
                total = total + axial[upper, plane(n * comps + m)] * given[n]
            add_plane(k, a, m, total)

    def fix_upper(k):
        rim_copy(k, 1).wait_recv()
        fix_layer(k, 1, [rim_in[k, 1, n] for n in range(comps)])

    def fix_lower(k):
        rim_copy(k, 0).wait_recv()
        fix_layer(k, 0, [rim_in[k, 0, n] for n in range(comps)])

    def relay(k):
        for step in range(highs):
            row_arrival(k, step).wait_recv()
        for step in list(range(1, lows)) + [0]:
            if step:
                forward[k, step] = rows[k][chosen[step]]
                forward_copy(k, step).start()
            else:
                picked[k][low] = rows[k][chosen[step]]

    def relay_cross():
        for step in range(highs):
            cross_arrival(step).wait_recv()
        for step in list(range(1, lows)) + [0]:
            if step:
                cross_forward[step] = cross[chosen[step]]
                cross_forward_copy(step).start()
            else:
                cross_picked[low] = cross[chosen[step]]

    def got(k, j, n, c):
        return picked[k][slots[j], n, c : c + 1, :]

    def crossing(k):
        def one(j, side, other, c):
            total = None
            for n in range(comps):
                start = side * pairs + n * comps
                term = cross_picked[slots[j], start : start + comps, :] * got(k - 1, other, n, c)
                total = term if total is None else total + term
            return total

        return one(1, 1, 0, around - 1), one(1, 0, 2, 0), one(2, 1, 1, around - 1)

    def facing_of(k, extra):
        values = []
        for n in range(comps):
            total = blend[plane(around)] * got(k, 2, n, 0)
            for c in range(around):
                total = total + blend[plane(c)] * got(k, 1, n, c)
            if extra is not None:
                begin, end, next_begin = extra
                total = total + blend[plane(0)] * begin[n : n + 1] + blend[plane(around - 1)] * end[n : n + 1]
                total = total + blend[plane(around)] * next_begin[n : n + 1]
            values.append(total)
        return values

    def complete_parts(k):
        i = k // 2
        mixing = pairs * layers + pairs
        for s in range(2):
            most, last = (0, 1) if s == 0 else (2, 3)
            ratios = coef_in[s, pl.ds(mixing, around)]
            ratio = coef_in[s, pl.ds(mixing + around, 1)]
            total = part_in[i, s, pl.ds(0, comps, stride=layers)]
            for n in range(comps):
                value = jnp.sum(ratios * picked[k][slots[most], n], axis=0, keepdims=True) + ratio * got(k, last, n, 0)
                total = total + coef_in[s, pl.ds(pairs * layers + n * comps, comps)] * value
            part_in[i, s, pl.ds(0, comps, stride=layers)] = total

    def wait_forward(k):
        for step in range(1, lows):
            forward_arrival(k, step).wait_recv()

    for side in range(2):
        coef_copy(side).start()

    @pl.when(is_rotor_face)
    def _():
        for side in range(2):
            for n in range(comps):
                cross_out[pl.ds(side * pairs + n * comps, comps)] = coef[
                    side, pl.ds(n * comps * layers + layers - 1, comps, stride=layers)
                ]
        for step in far_first:
            cross_copy(step).start()

    for k in range(ITERS):
        last = k == ITERS - 1
        even = k % 2 == 0
        make_radial(k)
        local_parts(k, 0, layers)
        if last:
            for m in range(comps):
                update_ref[m] = field[k, m, pl.ds(around, layers * around)]

        @pl.when(has_lower)
        def _():
            fix_lower(k)

        if even:

            @pl.when(block < blocks - 1)
            def _():
                fix_upper(k)

            @pl.when(is_rotor_face)
            def _():
                for n in range(comps):
                    row_out[k // 2, n] = field[k + 1, n, plane(layers)]
                send_rows(k + 1)

            for side in range(2):
                for n in range(comps):
                    part[k // 2, side, item(n)] = field[k + 1, n, column_of(rims[side], around)]
                part_copy(k, side).start()

            @pl.when(is_stator_face)
            def _():
                relay(k)

            for side in range(2):
                edge_copy(k, side).wait_recv()
            fix_sides(k)

            @pl.when(is_stator_face)
            def _():
                if k == 0:
                    relay_cross()
                relay(k + 1)
                wait_forward(k)
                fix_layer(k, 0, facing_of(k, None))

            send_rims(k + 1)
        else:

            @pl.when(is_stator_face)
            def _():
                if k == 1:
                    for step in range(1, lows):
                        cross_forward_arrival(step).wait_recv()

            for side in range(2):
                if k == 1:
                    coef_copy(side).wait_recv()
                part_copy(k, side).wait_recv()

            @pl.when(is_stator_face)
            def _():
                complete_parts(k - 1)

            fix_sides(k)

            @pl.when(block < blocks - 1)
            def _():
                fix_upper(k)

            @pl.when(is_stator_face)
            def _():
                extra = crossing(k)
                wait_forward(k)
                fix_layer(k, 0, facing_of(k, extra))

            if not last:

                @pl.when(is_rotor_face)
                def _():
                    send_rows(k + 1)

                send_rims(k + 1)
                take_edges(k + 1)
                for side in range(2):
                    edge_copy(k + 1, side).start()

    for side in range(2):
        coef_copy(side).wait_send()
        for k in (0, 2):
            edge_copy(k, side).wait_send()
            part_copy(k, side).wait_send()
    for k in range(ITERS):

        @pl.when(block > 0)
        def _():
            rim_copy(k, 1).wait_send()

        @pl.when(has_upper)
        def _():
            rim_copy(k, 0).wait_send()

        @pl.when(is_rotor_face)
        def _():
            for step in range(highs):
                row_copy(k, step).wait_send()

        @pl.when(is_stator_face)
        def _():
            for step in range(1, lows):
                forward_copy(k, step).wait_send()

    @pl.when(is_rotor_face)
    def _():
        for step in range(highs):
            cross_copy(step).wait_send()

    @pl.when(is_stator_face)
    def _():
        for step in range(1, lows):
            cross_forward_copy(step).wait_send()


UNROLL = 2


def solution(mesh):
    sectors, blocks = mesh.shape["sector"], mesh.shape["block"]
    lows = low_part(sectors)
    highs = sectors // lows

    def sweeps(prev, source, face, inverse, offset, cells, weights):
        comps, layers, around, lanes = prev.shape
        f32, dma = jnp.float32, pltpu.SemaphoreType.DMA
        flat = (comps, layers * around, lanes)
        pairs = comps * comps
        row = (comps, around, lanes)
        cross = (2 * pairs, lanes)
        sides = (2, 2, comps * layers, lanes)
        coefs = (2, pairs * layers + pairs + around + 1, lanes)
        hbm = pl.BlockSpec(memory_space=pl.ANY)
        vmem = pl.BlockSpec(memory_space=pltpu.VMEM)
        negative, previous = pl.pallas_call(
            functools.partial(kernel, sectors, blocks, layers, around),
            out_shape=(pltpu.VMEM(flat, f32),) * 2,
            in_specs=[hbm] * 7,
            out_specs=(vmem, vmem),
            scratch_shapes=[
                pltpu.SMEM(offset.shape, offset.dtype),
                pltpu.SMEM(cells.shape, cells.dtype),
                pltpu.SMEM(weights.shape, weights.dtype),
                pltpu.VMEM((ITERS, comps, (layers + 2) * around, lanes), f32),
                pltpu.VMEM(flat, f32),
                pltpu.VMEM(face.shape, face.dtype),
                pltpu.VMEM(inverse.shape, inverse.dtype),
                pltpu.VMEM((3, comps) + flat, f32),
                pltpu.VMEM((comps,) + flat, f32),
                pltpu.VMEM(flat, f32),
                pltpu.VMEM(sides, f32),
                pltpu.VMEM(sides, f32),
                pltpu.VMEM(sides, f32),
                pltpu.VMEM(sides, f32),
                pltpu.VMEM(coefs, f32),
                pltpu.VMEM(coefs, f32),
                pltpu.VMEM((2, pairs * around, lanes), f32),
                pltpu.VMEM((ITERS, 2) + row, f32),
                pltpu.VMEM((2,) + row, f32),
                [pltpu.VMEM((highs,) + row, f32)] * ITERS,
                pltpu.VMEM((ITERS, lows) + row, f32),
                [pltpu.VMEM((lows,) + row, f32)] * ITERS,
                pltpu.VMEM(cross, f32),
                pltpu.VMEM((highs,) + cross, f32),
                pltpu.VMEM((lows,) + cross, f32),
                pltpu.VMEM((lows,) + cross, f32),
                pltpu.VMEM(((around + 1) * around, lanes), f32),
                dma((7,)),
                dma((2, 2)),
                dma((2, 2)),
                dma((2, 2)),
                dma((2, 2)),
                dma((2,)),
                dma((2,)),
                dma((ITERS, 2)),
                dma((ITERS, 2)),
                dma((ITERS, highs)),
                dma((ITERS, highs)),
                dma((ITERS, lows)),
                dma((ITERS, lows)),
                dma((highs,)),
                dma((highs,)),
                dma((lows,)),
                dma((lows,)),
            ],
            compiler_params=pltpu.CompilerParams(collective_id=0, has_side_effects=True),
        )(prev.reshape(flat), source.reshape(flat), face, inverse, offset, cells, weights)
        negative, previous = negative.reshape(prev.shape), previous.reshape(prev.shape)
        return 0.0 - negative, 0.0 - negative - previous

    return jax.shard_map(
        sweeps,
        mesh=mesh,
        in_specs=(
            P(None, "block", "sector", None),
            P(None, "block", "sector", None),
            P(None, None, None, "block", "sector", None),
            P(None, None, "block", "sector", None),
            P(),
            P("sector"),
            P("sector"),
        ),
        out_specs=(P(None, "block", "sector", None), P(None, "block", "sector", None)),
        check_vma=False,
    )
```

time: 30.3 us -> 27.1 us (0.89)
  Pallas kernels: 28.1 us -> 24.9 us
    pallas_call x1, Pallas kernels: 28.1 us -> 24.9 us  [sweeps(): pl.pallas_call(functools.partial(kernel, sectors, blocks, layers, around)...]
where the time goes in v1:
time: 27.1 us; the launch traced here: 27 us
  Pallas kernels  24.9 us (92%)
  between operations  1.29 us (5%)
  other arithmetic  0.75 us (3%)
    pallas_call x1, Pallas kernels, sweeps(): pl.pallas_call(functools.partial(kernel, sectors, blocks, layers, around)...  24.9 us
    sub x1, other arithmetic, sweeps(): return (0.0 - negative, 0.0 - negative - previous)  0.75 us

profile of v1, /device:TPU:1, one launch (start us, length us, event | category | flops | bytes accessed | tf_op | source)
XLA Modules:
  0.0 27.0 jit_solution(1645565665499150260)
XLA Ops:
  1.3 24.9 %shard_map.86 = (f32[5,64,128]{2,1,0:T(8,128)S(1)}, f32[5,64,128]{2,1,0:T(8,128)S(1)}) custom-call(f32[5,64,128]{2,1,0:T(8,128)} %bitcast.7, f32[5,64,128]{2,1,0:T(8,128)} %bitcast.8, bf16[3,5,5,8,8,128]{5,4,3,2,1,0:T(8,128)(2,1)} %face_ref.1, bf16[5,5,8,8,128]{4,3,2,1,0:T(8,128)(2,1)} %inverse_ref.1, s32[1]{0:T(128)S(6)} %copy.9.offset_hbm, s32[8]{0:T(128)} %cells_hbm.1, ...), custom_call_target="tpu_custom_call" | custom-call | tf_op jit(solution)/shard_map/pallas_call | solution.py:637
  26.2 0.7 %bitcast_subtract_fusion = (f32[5,8,8,128]{3,2,1,0:T(8,128)}, f32[5,8,8,128]{3,2,1,0:T(8,128)}) fusion(f32[5,64,128]{2,1,0:T(8,128)S(1)} %get-tuple-element.5, f32[5,64,128]{2,1,0:T(8,128)S(1)} %get-tuple-element.4), kind=kLoop, calls=%fused_computation | loop fusion | flops 81920 | bytes 655360 | tf_op jit(solution)/shard_map/sub | solution.py:691

commit v2 on v1

--- a/solution.py
+++ b/solution.py
@@ -46,6 +46,9 @@
     part_in,
     coef,
     coef_in,
+    near,
+    near_in,
+    near_halo,
     axial,
     rim_in,
     row_out,
@@ -58,12 +61,15 @@
     cross_picked,
     blend,
     local_sem,
+    ready,
     edge_send,
     edge_recv,
     part_send,
     part_recv,
     coef_send,
     coef_recv,
+    near_send,
+    near_recv,
     rim_send,
     rim_recv,
     row_send,
@@ -77,6 +83,7 @@
 ):
     comps, _, lanes = prev_ref.shape
     pairs = comps * comps
+    mixing = comps + 2 * pairs
     sector = lax.axis_index("sector")
     block = lax.axis_index("block")
     first = blocks // 2
@@ -95,7 +102,13 @@
     def greet(to_sector, to_block):
         pl.semaphore_signal(barrier, inc=1, device_id=(to_sector, to_block), device_id_type=MESH)
 
-    greet(after, block)
+    is_end = sector == sectors - 1
+    is_start = sector == 0
+
+    @pl.when(~is_end)
+    def _():
+        greet(after, block)
+
     greet(before, block)
 
     @pl.when(block > 0)
@@ -137,6 +150,14 @@
     scalars = (into_offset, into_cells, into_weights)
     for copy in (into_field,) + scalars + (into_inverse, into_face, into_source):
         copy.start()
+
+    greetings = 2 - is_start.astype(jnp.int32) + (block > 0).astype(jnp.int32) + (block < blocks - 1).astype(jnp.int32)
+    greetings += jnp.where(is_rotor_face, highs, 0) + jnp.where(is_stator_face, highs + lows - 1, 0)
+
+    @pl.when(is_end)
+    def _():
+        pl.semaphore_wait(barrier, greetings)
+        pl.semaphore_signal(ready, inc=1, device_id=(after, block), device_id_type=MESH)
 
     nothing = jnp.zeros((around, lanes), jnp.float32)
     for k in range(ITERS):
@@ -171,10 +192,13 @@
 
     into_field.wait()
 
+    def slot_of(k):
+        return (0, 2, 1)[k]
+
     def take_edges(k):
         for side in range(2):
             for n in range(comps):
-                edge[k // 2, side, item(n)] = field[k, n, column_of(rims[side], around)]
+                edge[slot_of(k), side, item(n)] = field[k, n, column_of(rims[side], around)]
 
     take_edges(0)
 
@@ -187,7 +211,7 @@
         return (before if side else after, block)
 
     def edge_copy(k, side):
-        i = k // 2
+        i = slot_of(k)
         return remote(edge.at[i, side], halo.at[i, side], edge_send.at[i, side], edge_recv.at[i, side], beside(side))
 
     def part_copy(k, side):
@@ -196,6 +220,9 @@
 
     def coef_copy(side):
         return remote(coef.at[side], coef_in.at[side], coef_send.at[side], coef_recv.at[side], beside(side))
+
+    def near_copy(side):
+        return remote(near.at[side], near_in.at[side], near_send.at[side], near_recv.at[side], beside(side))
 
     def rim_copy(k, side):
         return remote(
@@ -262,12 +289,15 @@
         def _():
             rim_copy(k, 0).start()
 
-    greetings = 2 + (block > 0).astype(jnp.int32) + (block < blocks - 1).astype(jnp.int32)
-    greetings += jnp.where(is_rotor_face, highs, 0) + jnp.where(is_stator_face, highs + lows - 1, 0)
-    pl.semaphore_wait(barrier, greetings)
+    @pl.when(~is_end)
+    def _():
+        pl.semaphore_wait(barrier, greetings)
 
     edge_copy(0, 0).start()
-    edge_copy(0, 1).start()
+
+    @pl.when(~is_start)
+    def _():
+        edge_copy(0, 1).start()
 
     @pl.when(is_rotor_face)
     def _():
@@ -307,25 +337,38 @@
 
         lax.fori_loop(0, comps, body, 0)
 
+    for side in range(2):
+
+        def keep(i, value):
+            coef[side, pl.ds(pl.multiple_of(i * layers, layers), layers)] = value
+
+        product(1, column_of(rims[side]), LOWER if side else UPPER, keep)
+
+    @pl.when(is_rotor_face)
+    def _():
+        for side in range(2):
+            for n in range(comps):
+                cross_out[pl.ds(side * pairs + n * comps, comps)] = coef[
+                    side, pl.ds(n * comps * layers + layers - 1, comps, stride=layers)
+                ]
+
     for side, (a, share) in enumerate(((0, LOWER), (layers - 1, UPPER))):
 
         def keep(i, value):
             axial[side, pl.ds(pl.multiple_of(i * around, around), around)] = value
 
         product(0, plane(a), share, keep)
-    for side in range(2):
-
-        def keep(i, value):
-            coef[side, pl.ds(pl.multiple_of(i * layers, layers), layers)] = value
-
-        product(1, column_of(rims[side]), LOWER if side else UPPER, keep)
-        for n in range(comps):
-            coef[side, pl.ds(pairs * layers + n * comps, comps)] = axial[
-                0, pl.ds(n * comps * around + rims[side], comps, stride=around)
-            ]
-        mixing = pairs * layers + pairs
-        coef[side, pl.ds(mixing, around)] = blend[pl.ds(rims[side], around, stride=around)]
-        coef[side, pl.ds(mixing + around, 1)] = blend[pl.ds(around * around + rims[side], 1)]
+
+    @pl.when(is_stator_face)
+    def _():
+        for side in range(2):
+            for n in range(comps):
+                near[side, pl.ds(comps + n * comps, comps)] = coef[side, pl.ds(n * comps * layers, comps, stride=layers)]
+                near[side, pl.ds(comps + pairs + n * comps, comps)] = axial[
+                    0, pl.ds(n * comps * around + rims[side], comps, stride=around)
+                ]
+            near[side, pl.ds(mixing, around)] = blend[pl.ds(rims[side], around, stride=around)]
+            near[side, pl.ds(mixing + around, 1)] = blend[pl.ds(around * around + rims[side], 1)]
 
     into_source.wait()
 
@@ -356,6 +399,12 @@
             else:
                 adjoint_ref[m, plane(a)] = 0.0 - fresh
 
+    def send_parts(k):
+        for side in range(2):
+            for n in range(comps):
+                part[k // 2, side, item(n)] = field[k + 1, n, column_of(rims[side], around)]
+            part_copy(k, side).start()
+
     def local_parts(k, start, stop):
         def body(a, carry):
             local_part(k, a)
@@ -363,9 +412,10 @@
 
         lax.fori_loop(start, stop, body, 0, unroll=UNROLL)
 
-    def add_column(k, side, m, value):
+    def add_column(k, side, m, value, skip=0):
         if k < ITERS - 1:
-            where = column_of(rims[side], around)
+            where = pl.ds((1 + skip) * around + rims[side], layers - skip, stride=around)
+            value = value[skip:]
             field[k + 1, m, where] = field[k + 1, m, where] + value
         else:
             where = column_of(rims[side])
@@ -377,10 +427,8 @@
         else:
             adjoint_ref[m, plane(a)] = adjoint_ref[m, plane(a)] - value
 
-    def halo_of(k, s):
+    def completed(k, s):
         i = k // 2
-        if k % 2 == 0:
-            return [halo[i, s, item(n)] for n in range(comps)]
         own = [edge[i, 1 - s, item(n)] for n in range(comps)]
         values = []
         for m in range(comps):
@@ -390,14 +438,17 @@
             values.append(total)
         return values
 
-    def fix_sides(k):
+    def received(k, s):
+        return [halo[slot_of(k), s, item(n)] for n in range(comps)]
+
+    def fix_sides(k, halo_of, skip=0):
         for side in range(2):
             given = halo_of(k, 1 - side)
             for m in range(comps):
                 total = coef[side, item(m)] * given[0]
                 for n in range(1, comps):
                     total = total + coef[side, item(n * comps + m)] * given[n]
-                add_column(k, side, m, total)
+                add_column(k, side, m, total, skip)
 
     def fix_layer(k, upper, given):
         a = layers - 1 if upper else 0
@@ -462,35 +513,80 @@
             values.append(total)
         return values
 
+    def facing_beside(k, s):
+        most, last = (0, 1) if s == 0 else (2, 3)
+        ratios = near_in[s, pl.ds(mixing, around)]
+        ratio = near_in[s, pl.ds(mixing + around, 1)]
+        total = None
+        for n in range(comps):
+            value = jnp.sum(ratios * picked[k][slots[most], n], axis=0, keepdims=True) + ratio * got(k, last, n, 0)
+            term = near_in[s, pl.ds(comps + pairs + n * comps, comps)] * value
+            total = term if total is None else total + term
+        return total
+
     def complete_parts(k):
-        i = k // 2
-        mixing = pairs * layers + pairs
         for s in range(2):
-            most, last = (0, 1) if s == 0 else (2, 3)
-            ratios = coef_in[s, pl.ds(mixing, around)]
-            ratio = coef_in[s, pl.ds(mixing + around, 1)]
-            total = part_in[i, s, pl.ds(0, comps, stride=layers)]
+            where = pl.ds(0, comps, stride=layers)
+            part_in[k // 2, s, where] = part_in[k // 2, s, where] + facing_beside(k, s)
+
+    def complete_near():
+        for s in range(2):
+            total = near_in[s, pl.ds(0, comps)] + facing_beside(0, s)
             for n in range(comps):
-                value = jnp.sum(ratios * picked[k][slots[most], n], axis=0, keepdims=True) + ratio * got(k, last, n, 0)
-                total = total + coef_in[s, pl.ds(pairs * layers + n * comps, comps)] * value
-            part_in[i, s, pl.ds(0, comps, stride=layers)] = total
+                total = total + near_in[s, pl.ds(comps + n * comps, comps)] * edge[0, 1 - s, pl.ds(n * layers, 1)]
+            near_halo[s] = total
+
+    def fix_near():
+        for side in range(2):
+            total = None
+            for n in range(comps):
+                term = near[side, pl.ds(comps + n * comps, comps)] * near_halo[1 - side, pl.ds(n, 1)]
+                total = term if total is None else total + term
+            for m in range(comps):
+                where = pl.ds(around + rims[side], 1)
+                field[2, m, where] = field[2, m, where] + total[m : m + 1]
 
     def wait_forward(k):
         for step in range(1, lows):
             forward_arrival(k, step).wait_recv()
 
-    for side in range(2):
-        coef_copy(side).start()
-
-    @pl.when(is_rotor_face)
-    def _():
+    def wait_sends():
         for side in range(2):
-            for n in range(comps):
-                cross_out[pl.ds(side * pairs + n * comps, comps)] = coef[
-                    side, pl.ds(n * comps * layers + layers - 1, comps, stride=layers)
-                ]
-        for step in far_first:
-            cross_copy(step).start()
+            coef_copy(side).wait_send()
+            edge_copy(0, side).wait_send()
+            edge_copy(2, side).wait_send()
+            part_copy(2, side).wait_send()
+        for k in range(ITERS):
+
+            @pl.when(block > 0)
+            def _():
+                rim_copy(k, 1).wait_send()
+
+            @pl.when(has_upper)
+            def _():
+                rim_copy(k, 0).wait_send()
+
+        @pl.when(is_rotor_face)
+        def _():
+            for step in range(highs):
+                cross_copy(step).wait_send()
+                for k in range(ITERS):
+                    row_copy(k, step).wait_send()
+
+        @pl.when(is_stator_face)
+        def _():
+            for side in range(2):
+                near_copy(side).wait_send()
+                edge_copy(1, side).wait_send()
+            for step in range(1, lows):
+                cross_forward_copy(step).wait_send()
+                for k in range(ITERS):
+                    forward_copy(k, step).wait_send()
+
+        @pl.when(~is_stator_face)
+        def _():
+            for side in range(2):
+                part_copy(0, side).wait_send()
 
     for k in range(ITERS):
         last = k == ITERS - 1
@@ -516,11 +612,32 @@
                 for n in range(comps):
                     row_out[k // 2, n] = field[k + 1, n, plane(layers)]
                 send_rows(k + 1)
-
-            for side in range(2):
-                for n in range(comps):
-                    part[k // 2, side, item(n)] = field[k + 1, n, column_of(rims[side], around)]
-                part_copy(k, side).start()
+                if k == 0:
+                    for step in far_first:
+                        cross_copy(step).start()
+
+            if k == 0:
+
+                @pl.when(is_start)
+                def _():
+                    pl.semaphore_wait(ready, 1)
+                    edge_copy(0, 1).start()
+
+                @pl.when(is_stator_face)
+                def _():
+                    for side in range(2):
+                        for m in range(comps):
+                            near[side, pl.ds(m, 1)] = field[1, m, pl.ds(around + rims[side], 1)]
+                        near_copy(side).start()
+
+                @pl.when(~is_stator_face)
+                def _():
+                    send_parts(0)
+                    for side in range(2):
+                        coef_copy(side).start()
+
+            else:
+                send_parts(k)
 
             @pl.when(is_stator_face)
             def _():
@@ -528,35 +645,83 @@
 
             for side in range(2):
                 edge_copy(k, side).wait_recv()
-            fix_sides(k)
+            fix_sides(k, received)
 
             @pl.when(is_stator_face)
             def _():
+                if k == 0:
+                    take_edges(1)
+                    for side in range(2):
+                        edge_copy(1, side).start()
+                relay(k + 1)
                 if k == 0:
                     relay_cross()
-                relay(k + 1)
+                    for side in range(2):
+                        coef_copy(side).start()
+                        near_copy(side).wait_recv()
                 wait_forward(k)
                 fix_layer(k, 0, facing_of(k, None))
 
             send_rims(k + 1)
+        elif not last:
+
+            @pl.when(is_stator_face)
+            def _():
+                complete_near()
+                fix_near()
+                for step in range(1, lows):
+                    cross_forward_arrival(step).wait_recv()
+                extra = crossing(k)
+
+                @pl.when(block < blocks - 1)
+                def _():
+                    fix_upper(k)
+
+                wait_forward(k)
+                fix_layer(k, 0, facing_of(k, extra))
+                rim_copy(k + 1, 1).start()
+                for side in range(2):
+                    edge_copy(1, side).wait_recv()
+                fix_sides(k, received, 1)
+
+            @pl.when(~is_stator_face)
+            def _():
+                for side in range(2):
+                    part_copy(0, side).wait_recv()
+                    coef_copy(side).wait_recv()
+                fix_sides(k, completed)
+
+                @pl.when(block < blocks - 1)
+                def _():
+                    fix_upper(k)
+
+                @pl.when(is_rotor_face)
+                def _():
+                    send_rows(k + 1)
+
+                @pl.when(block > 0)
+                def _():
+                    rim_copy(k + 1, 1).start()
+
+            @pl.when(has_upper)
+            def _():
+                rim_copy(k + 1, 0).start()
+
+            take_edges(k + 1)
+            for side in range(2):
+                edge_copy(k + 1, side).start()
         else:
+            for side in range(2):
+                part_copy(k, side).wait_recv()
 
             @pl.when(is_stator_face)
             def _():
-                if k == 1:
-                    for step in range(1, lows):
-                        cross_forward_arrival(step).wait_recv()
-
-            for side in range(2):
-                if k == 1:
+                for side in range(2):
                     coef_copy(side).wait_recv()
-                part_copy(k, side).wait_recv()
-
-            @pl.when(is_stator_face)
-            def _():
                 complete_parts(k - 1)
 
-            fix_sides(k)
+            fix_sides(k, completed)
+            wait_sends()
 
             @pl.when(block < blocks - 1)
             def _():
@@ -567,52 +732,6 @@
                 extra = crossing(k)
                 wait_forward(k)
                 fix_layer(k, 0, facing_of(k, extra))
-
-            if not last:
-
-                @pl.when(is_rotor_face)
-                def _():
-                    send_rows(k + 1)
-
-                send_rims(k + 1)
-                take_edges(k + 1)
-                for side in range(2):
-                    edge_copy(k + 1, side).start()
-
-    for side in range(2):
-        coef_copy(side).wait_send()
-        for k in (0, 2):
-            edge_copy(k, side).wait_send()
-            part_copy(k, side).wait_send()
-    for k in range(ITERS):
-
-        @pl.when(block > 0)
-        def _():
-            rim_copy(k, 1).wait_send()
-
-        @pl.when(has_upper)
-        def _():
-            rim_copy(k, 0).wait_send()
-
-        @pl.when(is_rotor_face)
-        def _():
-            for step in range(highs):
-                row_copy(k, step).wait_send()
-
-        @pl.when(is_stator_face)
-        def _():
-            for step in range(1, lows):
-                forward_copy(k, step).wait_send()
-
-    @pl.when(is_rotor_face)
-    def _():
-        for step in range(highs):
-            cross_copy(step).wait_send()
-
-    @pl.when(is_stator_face)
-    def _():
-        for step in range(1, lows):
-            cross_forward_copy(step).wait_send()
 
 
 UNROLL = 2
@@ -630,8 +749,8 @@
         pairs = comps * comps
         row = (comps, around, lanes)
         cross = (2 * pairs, lanes)
-        sides = (2, 2, comps * layers, lanes)
-        coefs = (2, pairs * layers + pairs + around + 1, lanes)
+        sides = (2, comps * layers, lanes)
+        near = (2, comps + 2 * pairs + around + 1, lanes)
         hbm = pl.BlockSpec(memory_space=pl.ANY)
         vmem = pl.BlockSpec(memory_space=pltpu.VMEM)
         negative, previous = pl.pallas_call(
@@ -650,12 +769,15 @@
                 pltpu.VMEM((3, comps) + flat, f32),
                 pltpu.VMEM((comps,) + flat, f32),
                 pltpu.VMEM(flat, f32),
-                pltpu.VMEM(sides, f32),
-                pltpu.VMEM(sides, f32),
-                pltpu.VMEM(sides, f32),
-                pltpu.VMEM(sides, f32),
-                pltpu.VMEM(coefs, f32),
-                pltpu.VMEM(coefs, f32),
+                pltpu.VMEM((3,) + sides, f32),
+                pltpu.VMEM((3,) + sides, f32),
+                pltpu.VMEM((2,) + sides, f32),
+                pltpu.VMEM((2,) + sides, f32),
+                pltpu.VMEM((2, pairs * layers, lanes), f32),
+                pltpu.VMEM((2, pairs * layers, lanes), f32),
+                pltpu.VMEM(near, f32),
+                pltpu.VMEM(near, f32),
+                pltpu.VMEM((2, comps, lanes), f32),
                 pltpu.VMEM((2, pairs * around, lanes), f32),
                 pltpu.VMEM((ITERS, 2) + row, f32),
                 pltpu.VMEM((2,) + row, f32),
@@ -668,10 +790,13 @@
                 pltpu.VMEM((lows,) + cross, f32),
                 pltpu.VMEM(((around + 1) * around, lanes), f32),
                 dma((7,)),
+                pltpu.SemaphoreType.REGULAR,
+                dma((3, 2)),
+                dma((3, 2)),
                 dma((2, 2)),
                 dma((2, 2)),
-                dma((2, 2)),
-                dma((2, 2)),
+                dma((2,)),
+                dma((2,)),
                 dma((2,)),
                 dma((2,)),
                 dma((ITERS, 2)),

time: 27.1 us -> 25.7 us (0.948)
  Pallas kernels: 24.9 us -> 23.5 us
    pallas_call x1, Pallas kernels: 24.9 us -> 23.5 us  [sweeps(): pl.pallas_call(functools.partial(kernel, sectors, blocks, layers, around)...]
where the time goes in v2:
time: 25.7 us; the launch traced here: 25.5 us
  Pallas kernels  23.5 us (91%)
  between operations  1.29 us (5%)
  other arithmetic  0.75 us (3%)
    pallas_call x1, Pallas kernels, sweeps(): pl.pallas_call(functools.partial(kernel, sectors, blocks, layers, around)...  23.5 us
    sub x1, other arithmetic, sweeps(): return (0.0 - negative, 0.0 - negative - previous)  0.75 us

profile of v2, /device:TPU:1, one launch (start us, length us, event | category | flops | bytes accessed | tf_op | source)
XLA Modules:
  0.0 25.5 jit_solution(11935842007575308603)
XLA Ops:
  1.3 23.5 %shard_map.86 = (f32[5,64,128]{2,1,0:T(8,128)S(1)}, f32[5,64,128]{2,1,0:T(8,128)S(1)}) custom-call(f32[5,64,128]{2,1,0:T(8,128)} %bitcast.7, f32[5,64,128]{2,1,0:T(8,128)} %bitcast.8, bf16[3,5,5,8,8,128]{5,4,3,2,1,0:T(8,128)(2,1)} %face_ref.1, bf16[5,5,8,8,128]{4,3,2,1,0:T(8,128)(2,1)} %inverse_ref.1, s32[1]{0:T(128)S(6)} %copy.9.offset_hbm, s32[8]{0:T(128)} %cells_hbm.1, ...), custom_call_target="tpu_custom_call" | custom-call | tf_op jit(solution)/shard_map/pallas_call | solution.py:756
  24.8 0.7 %bitcast_subtract_fusion = (f32[5,8,8,128]{3,2,1,0:T(8,128)}, f32[5,8,8,128]{3,2,1,0:T(8,128)}) fusion(f32[5,64,128]{2,1,0:T(8,128)S(1)} %get-tuple-element.5, f32[5,64,128]{2,1,0:T(8,128)S(1)} %get-tuple-element.4), kind=kLoop, calls=%fused_computation | loop fusion | flops 81920 | bytes 655360 | tf_op jit(solution)/shard_map/sub | solution.py:816

commit v3 on v2

--- a/solution.py
+++ b/solution.py
@@ -212,24 +212,24 @@
 
     def edge_copy(k, side):
         i = slot_of(k)
-        return remote(edge.at[i, side], halo.at[i, side], edge_send.at[i, side], edge_recv.at[i, side], beside(side))
+        return remote(edge.at[i, side], halo.at[i, side], edge_send.at[i], edge_recv.at[i], beside(side))
 
     def part_copy(k, side):
         i = k // 2
-        return remote(part.at[i, side], part_in.at[i, side], part_send.at[i, side], part_recv.at[i, side], beside(side))
+        return remote(part.at[i, side], part_in.at[i, side], part_send.at[i], part_recv.at[i], beside(side))
 
     def coef_copy(side):
         return remote(coef.at[side], coef_in.at[side], coef_send.at[side], coef_recv.at[side], beside(side))
 
     def near_copy(side):
-        return remote(near.at[side], near_in.at[side], near_send.at[side], near_recv.at[side], beside(side))
+        return remote(near.at[side], near_in.at[side], near_send, near_recv, beside(side))
 
     def rim_copy(k, side):
         return remote(
             field.at[k, :, plane(1 if side else layers)],
             rim_in.at[k, side],
-            rim_send.at[k, side],
-            rim_recv.at[k, side],
+            rim_send.at[k, 1 - side],
+            rim_recv.at[k, 1 - side],
             (sector, block - 1 if side else block + 1),
         )
 
@@ -238,41 +238,46 @@
 
     def row_copy(k, step):
         to = (high + step) % highs
-        return remote(row_source(k), rows[k].at[high], row_send.at[k, step], row_recv.at[k, step], (to * lows + low, first))
-
-    def row_arrival(k, step):
-        origin = (high + highs - step) % highs
-        return remote(row_source(k), rows[k].at[origin], row_send.at[k, step], row_recv.at[k, step], (origin * lows + low, first))
+        return remote(row_source(k), rows[k].at[high], row_send.at[k], row_recv.at[k], (to * lows + low, first))
+
+    def all_rows(k):
+        return remote(rows[k], rows[k], row_send.at[k], row_recv.at[k], (sector, first))
 
     def cross_copy(step):
         to = (high + step) % highs
-        return remote(cross_out, cross.at[high], cross_send.at[step], cross_recv.at[step], (to * lows + low, first))
-
-    def cross_arrival(step):
-        origin = (high + highs - step) % highs
-        return remote(cross_out, cross.at[origin], cross_send.at[step], cross_recv.at[step], (origin * lows + low, first))
+        return remote(cross_out, cross.at[high], cross_send, cross_recv, (to * lows + low, first))
+
+    def all_crosses():
+        return remote(cross, cross, cross_send, cross_recv, (sector, first))
 
     def forward_copy(k, step):
         to = (high * lows + (low + step) % lows, first)
-        return remote(forward.at[k, step], picked[k].at[low], forward_send.at[k, step], forward_recv.at[k, step], to)
-
-    def forward_arrival(k, step):
-        origin = (low + lows - step) % lows
-        to = (high * lows + origin, first)
-        return remote(forward.at[k, step], picked[k].at[origin], forward_send.at[k, step], forward_recv.at[k, step], to)
+        return remote(forward.at[k, step], picked[k].at[low], forward_send.at[k], forward_recv.at[k], to)
+
+    def all_forwards(k):
+        part = forward.at[k, pl.ds(1, lows - 1)]
+        return remote(part, part, forward_send.at[k], forward_recv.at[k], (sector, first))
 
     def cross_forward_copy(step):
         to = (high * lows + (low + step) % lows, first)
         return remote(
-            cross_forward.at[step], cross_picked.at[low], cross_forward_send.at[step], cross_forward_recv.at[step], to
+            cross_forward.at[step], cross_picked.at[low], cross_forward_send, cross_forward_recv, to
         )
 
-    def cross_forward_arrival(step):
-        origin = (low + lows - step) % lows
-        to = (high * lows + origin, first)
-        return remote(
-            cross_forward.at[step], cross_picked.at[origin], cross_forward_send.at[step], cross_forward_recv.at[step], to
-        )
+    def all_cross_forwards():
+        part = cross_forward.at[pl.ds(1, lows - 1)]
+        return remote(part, part, cross_forward_send, cross_forward_recv, (sector, first))
+
+    def both_edges(k):
+        i = slot_of(k)
+        return remote(edge.at[i], halo.at[i], edge_send.at[i], edge_recv.at[i], beside(0))
+
+    def both_parts(k):
+        i = k // 2
+        return remote(part.at[i], part_in.at[i], part_send.at[i], part_recv.at[i], beside(0))
+
+    def both_near():
+        return remote(near, near_in, near_send, near_recv, beside(0))
 
     far_first = sorted(range(highs), key=lambda step: -min(step, highs - step))
 
@@ -351,6 +356,8 @@
                 cross_out[pl.ds(side * pairs + n * comps, comps)] = coef[
                     side, pl.ds(n * comps * layers + layers - 1, comps, stride=layers)
                 ]
+        for step in far_first:
+            cross_copy(step).start()
 
     for side, (a, share) in enumerate(((0, LOWER), (layers - 1, UPPER))):
 
@@ -467,8 +474,7 @@
         fix_layer(k, 0, [rim_in[k, 0, n] for n in range(comps)])
 
     def relay(k):
-        for step in range(highs):
-            row_arrival(k, step).wait_recv()
+        all_rows(k).wait_recv()
         for step in list(range(1, lows)) + [0]:
             if step:
                 forward[k, step] = rows[k][chosen[step]]
@@ -477,8 +483,7 @@
                 picked[k][low] = rows[k][chosen[step]]
 
     def relay_cross():
-        for step in range(highs):
-            cross_arrival(step).wait_recv()
+        all_crosses().wait_recv()
         for step in list(range(1, lows)) + [0]:
             if step:
                 cross_forward[step] = cross[chosen[step]]
@@ -547,15 +552,14 @@
                 field[2, m, where] = field[2, m, where] + total[m : m + 1]
 
     def wait_forward(k):
-        for step in range(1, lows):
-            forward_arrival(k, step).wait_recv()
+        all_forwards(k).wait_recv()
 
     def wait_sends():
         for side in range(2):
             coef_copy(side).wait_send()
-            edge_copy(0, side).wait_send()
-            edge_copy(2, side).wait_send()
-            part_copy(2, side).wait_send()
+        both_edges(0).wait_send()
+        both_edges(2).wait_send()
+        both_parts(2).wait_send()
         for k in range(ITERS):
 
             @pl.when(block > 0)
@@ -568,25 +572,21 @@
 
         @pl.when(is_rotor_face)
         def _():
-            for step in range(highs):
-                cross_copy(step).wait_send()
-                for k in range(ITERS):
-                    row_copy(k, step).wait_send()
+            all_crosses().wait_send()
+            for k in range(ITERS):
+                all_rows(k).wait_send()
 
         @pl.when(is_stator_face)
         def _():
-            for side in range(2):
-                near_copy(side).wait_send()
-                edge_copy(1, side).wait_send()
-            for step in range(1, lows):
-                cross_forward_copy(step).wait_send()
-                for k in range(ITERS):
-                    forward_copy(k, step).wait_send()
+            both_near().wait_send()
+            both_edges(1).wait_send()
+            all_cross_forwards().wait_send()
+            for k in range(ITERS):
+                all_forwards(k).wait_send()
 
         @pl.when(~is_stator_face)
         def _():
-            for side in range(2):
-                part_copy(0, side).wait_send()
+            both_parts(0).wait_send()
 
     for k in range(ITERS):
         last = k == ITERS - 1
@@ -612,9 +612,6 @@
                 for n in range(comps):
                     row_out[k // 2, n] = field[k + 1, n, plane(layers)]
                 send_rows(k + 1)
-                if k == 0:
-                    for step in far_first:
-                        cross_copy(step).start()
 
             if k == 0:
 
@@ -643,8 +640,7 @@
             def _():
                 relay(k)
 
-            for side in range(2):
-                edge_copy(k, side).wait_recv()
+            both_edges(k).wait_recv()
             fix_sides(k, received)
 
             @pl.when(is_stator_face)
@@ -653,12 +649,13 @@
                     take_edges(1)
                     for side in range(2):
                         edge_copy(1, side).start()
+                if k == 0:
+                    relay_cross()
                 relay(k + 1)
                 if k == 0:
-                    relay_cross()
                     for side in range(2):
                         coef_copy(side).start()
-                        near_copy(side).wait_recv()
+                    both_near().wait_recv()
                 wait_forward(k)
                 fix_layer(k, 0, facing_of(k, None))
 
@@ -669,8 +666,7 @@
             def _():
                 complete_near()
                 fix_near()
-                for step in range(1, lows):
-                    cross_forward_arrival(step).wait_recv()
+                all_cross_forwards().wait_recv()
                 extra = crossing(k)
 
                 @pl.when(block < blocks - 1)
@@ -680,14 +676,13 @@
                 wait_forward(k)
                 fix_layer(k, 0, facing_of(k, extra))
                 rim_copy(k + 1, 1).start()
+                both_edges(1).wait_recv()
+                fix_sides(k, received, 1)
+
+            @pl.when(~is_stator_face)
+            def _():
+                both_parts(0).wait_recv()
                 for side in range(2):
-                    edge_copy(1, side).wait_recv()
-                fix_sides(k, received, 1)
-
-            @pl.when(~is_stator_face)
-            def _():
-                for side in range(2):
-                    part_copy(0, side).wait_recv()
                     coef_copy(side).wait_recv()
                 fix_sides(k, completed)
 
@@ -711,8 +706,7 @@
             for side in range(2):
                 edge_copy(k + 1, side).start()
         else:
-            for side in range(2):
-                part_copy(k, side).wait_recv()
+            both_parts(k).wait_recv()
 
             @pl.when(is_stator_face)
             def _():
@@ -791,24 +785,24 @@
                 pltpu.VMEM(((around + 1) * around, lanes), f32),
                 dma((7,)),
                 pltpu.SemaphoreType.REGULAR,
-                dma((3, 2)),
-                dma((3, 2)),
-                dma((2, 2)),
-                dma((2, 2)),
+                dma((3,)),
+                dma((3,)),
                 dma((2,)),
                 dma((2,)),
                 dma((2,)),
                 dma((2,)),
-                dma((ITERS, 2)),
-                dma((ITERS, 2)),
-                dma((ITERS, highs)),
-                dma((ITERS, highs)),
-                dma((ITERS, lows)),
-                dma((ITERS, lows)),
-                dma((highs,)),
-                dma((highs,)),
-                dma((lows,)),
-                dma((lows,)),
+                dma,
+                dma,
+                dma((ITERS, min(blocks - 1, 2))),
+                dma((ITERS, min(blocks - 1, 2))),
+                dma((ITERS,)),
+                dma((ITERS,)),
+                dma((ITERS,)),
+                dma((ITERS,)),
+                dma,
+                dma,
+                dma,
+                dma,
             ],
             compiler_params=pltpu.CompilerParams(collective_id=0, has_side_effects=True),
         )(prev.reshape(flat), source.reshape(flat), face, inverse, offset, cells, weights)

time: 25.7 us -> 24.6 us (0.957)
  Pallas kernels: 23.5 us -> 22.4 us
    pallas_call x1, Pallas kernels: 23.5 us -> 22.4 us  [sweeps(): pl.pallas_call(functools.partial(kernel, sectors, blocks, layers, around)...]
where the time goes in v3:
time: 24.6 us; the launch traced here: 24.5 us
  Pallas kernels  22.4 us (91%)
  between operations  1.29 us (5%)
  other arithmetic  0.75 us (3%)
    pallas_call x1, Pallas kernels, sweeps(): pl.pallas_call(functools.partial(kernel, sectors, blocks, layers, around)...  22.4 us
    sub x1, other arithmetic, sweeps(): return (0.0 - negative, 0.0 - negative - previous)  0.75 us

profile of v3, /device:TPU:1, one launch (start us, length us, event | category | flops | bytes accessed | tf_op | source)
XLA Modules:
  0.0 24.5 jit_solution(8085208785010190390)
XLA Ops:
  1.3 22.4 %shard_map.86 = (f32[5,64,128]{2,1,0:T(8,128)S(1)}, f32[5,64,128]{2,1,0:T(8,128)S(1)}) custom-call(f32[5,64,128]{2,1,0:T(8,128)} %bitcast.7, f32[5,64,128]{2,1,0:T(8,128)} %bitcast.8, bf16[3,5,5,8,8,128]{5,4,3,2,1,0:T(8,128)(2,1)} %face_ref.1, bf16[5,5,8,8,128]{4,3,2,1,0:T(8,128)(2,1)} %inverse_ref.1, s32[1]{0:T(128)S(6)} %copy.9.offset_hbm, s32[8]{0:T(128)} %cells_hbm.1, ...), custom_call_target="tpu_custom_call" | custom-call | tf_op jit(solution)/shard_map/pallas_call | solution.py:750
  23.7 0.7 %bitcast_subtract_fusion = (f32[5,8,8,128]{3,2,1,0:T(8,128)}, f32[5,8,8,128]{3,2,1,0:T(8,128)}) fusion(f32[5,64,128]{2,1,0:T(8,128)S(1)} %get-tuple-element.5, f32[5,64,128]{2,1,0:T(8,128)S(1)} %get-tuple-element.4), kind=kLoop, calls=%fused_computation | loop fusion | flops 81920 | bytes 655360 | tf_op jit(solution)/shard_map/sub | solution.py:810

commit v4 on v3

--- a/solution.py
+++ b/solution.py
@@ -97,6 +97,9 @@
     has_upper = (block < blocks - 1) & (block != first - 1)
     rims = (around - 1, 0)
 
+    def partner(step):
+        return low ^ step if lows & (lows - 1) == 0 else (low + step) % lows
+
     barrier = pltpu.get_barrier_semaphore()
 
     def greet(to_sector, to_block):
@@ -129,7 +132,7 @@
         for step in range(highs):
             greet(((high + step) % highs) * lows + low, first - 1)
         for step in range(1, lows):
-            greet(high * lows + (low + step) % lows, first)
+            greet(high * lows + partner(step), first)
 
     def plane(a):
         return pl.ds(a * around, around) if isinstance(a, int) else pl.ds(pl.multiple_of(a * around, around), around)
@@ -184,7 +187,7 @@
     offset = offset_ref[0]
     chosen = []
     for step in range(lows):
-        to = high * lows + (low + step) % lows
+        to = high * lows + partner(step)
         base = to + 2 * sectors - offset - 1
         ahead = lax.rem(low + lows - lax.rem(base, lows), lows)
         chosen.append(lax.rem(lax.div(base + ahead, lows), highs))
@@ -195,8 +198,8 @@
     def slot_of(k):
         return (0, 2, 1)[k]
 
-    def take_edges(k):
-        for side in range(2):
+    def take_edges(k, sides=(0, 1)):
+        for side in sides:
             for n in range(comps):
                 edge[slot_of(k), side, item(n)] = field[k, n, column_of(rims[side], around)]
 
@@ -212,14 +215,14 @@
 
     def edge_copy(k, side):
         i = slot_of(k)
-        return remote(edge.at[i, side], halo.at[i, side], edge_send.at[i], edge_recv.at[i], beside(side))
+        return remote(edge.at[i, side], halo.at[i, side], edge_send.at[i], edge_recv.at[i, side], beside(side))
 
     def part_copy(k, side):
         i = k // 2
         return remote(part.at[i, side], part_in.at[i, side], part_send.at[i], part_recv.at[i], beside(side))
 
     def coef_copy(side):
-        return remote(coef.at[side], coef_in.at[side], coef_send.at[side], coef_recv.at[side], beside(side))
+        return remote(coef.at[side], coef_in.at[side], coef_send, coef_recv, beside(side))
 
     def near_copy(side):
         return remote(near.at[side], near_in.at[side], near_send, near_recv, beside(side))
@@ -251,7 +254,7 @@
         return remote(cross, cross, cross_send, cross_recv, (sector, first))
 
     def forward_copy(k, step):
-        to = (high * lows + (low + step) % lows, first)
+        to = (high * lows + partner(step), first)
         return remote(forward.at[k, step], picked[k].at[low], forward_send.at[k], forward_recv.at[k], to)
 
     def all_forwards(k):
@@ -259,7 +262,7 @@
         return remote(part, part, forward_send.at[k], forward_recv.at[k], (sector, first))
 
     def cross_forward_copy(step):
-        to = (high * lows + (low + step) % lows, first)
+        to = (high * lows + partner(step), first)
         return remote(
             cross_forward.at[step], cross_picked.at[low], cross_forward_send, cross_forward_recv, to
         )
@@ -270,7 +273,7 @@
 
     def both_edges(k):
         i = slot_of(k)
-        return remote(edge.at[i], halo.at[i], edge_send.at[i], edge_recv.at[i], beside(0))
+        return remote(edge.at[i], halo.at[i], edge_send.at[i], edge_recv.at[i, 0], beside(0))
 
     def both_parts(k):
         i = k // 2
@@ -279,6 +282,7 @@
     def both_near():
         return remote(near, near_in, near_send, near_recv, beside(0))
 
+    near_last = sorted(range(lows), key=lambda step: -bin(step).count("1"))
     far_first = sorted(range(highs), key=lambda step: -min(step, highs - step))
 
     def send_rows(k):
@@ -298,17 +302,17 @@
     def _():
         pl.semaphore_wait(barrier, greetings)
 
+    send_rims(0)
+
+    @pl.when(is_rotor_face)
+    def _():
+        send_rows(0)
+
     edge_copy(0, 0).start()
 
     @pl.when(~is_start)
     def _():
         edge_copy(0, 1).start()
-
-    @pl.when(is_rotor_face)
-    def _():
-        send_rows(0)
-
-    send_rims(0)
 
     into_inverse.wait()
 
@@ -406,11 +410,10 @@
             else:
                 adjoint_ref[m, plane(a)] = 0.0 - fresh
 
-    def send_parts(k):
-        for side in range(2):
-            for n in range(comps):
-                part[k // 2, side, item(n)] = field[k + 1, n, column_of(rims[side], around)]
-            part_copy(k, side).start()
+    def send_part(k, side):
+        for n in range(comps):
+            part[k // 2, side, item(n)] = field[k + 1, n, column_of(rims[side], around)]
+        part_copy(k, side).start()
 
     def local_parts(k, start, stop):
         def body(a, carry):
@@ -445,17 +448,26 @@
             values.append(total)
         return values
 
+    def sent(k, s):
+        return [part_in[k // 2, s, item(n)] for n in range(comps)]
+
     def received(k, s):
         return [halo[slot_of(k), s, item(n)] for n in range(comps)]
 
-    def fix_sides(k, halo_of, skip=0):
-        for side in range(2):
-            given = halo_of(k, 1 - side)
-            for m in range(comps):
-                total = coef[side, item(m)] * given[0]
-                for n in range(1, comps):
-                    total = total + coef[side, item(n * comps + m)] * given[n]
-                add_column(k, side, m, total, skip)
+    def fix_side(k, side, halo_of, skip=0):
+        given = halo_of(k, 1 - side)
+        for m in range(comps):
+            total = coef[side, item(m)] * given[0]
+            for n in range(1, comps):
+                total = total + coef[side, item(n * comps + m)] * given[n]
+            add_column(k, side, m, total, skip)
+
+    def by_place(body):
+        for parity in range(2):
+
+            @pl.when(sector % 2 == parity)
+            def _():
+                body(1 - parity, parity)
 
     def fix_layer(k, upper, given):
         a = layers - 1 if upper else 0
@@ -475,7 +487,7 @@
 
     def relay(k):
         all_rows(k).wait_recv()
-        for step in list(range(1, lows)) + [0]:
+        for step in near_last:
             if step:
                 forward[k, step] = rows[k][chosen[step]]
                 forward_copy(k, step).start()
@@ -484,7 +496,7 @@
 
     def relay_cross():
         all_crosses().wait_recv()
-        for step in list(range(1, lows)) + [0]:
+        for step in near_last:
             if step:
                 cross_forward[step] = cross[chosen[step]]
                 cross_forward_copy(step).start()
@@ -555,8 +567,7 @@
         all_forwards(k).wait_recv()
 
     def wait_sends():
-        for side in range(2):
-            coef_copy(side).wait_send()
+        coef_copy(0).wait_send()
         both_edges(0).wait_send()
         both_edges(2).wait_send()
         both_parts(2).wait_send()
@@ -586,7 +597,11 @@
 
         @pl.when(~is_stator_face)
         def _():
-            both_parts(0).wait_send()
+            edge_copy(1, 0).wait_send()
+            part_copy(0, 0).wait_send()
+
+    def arrive(k, side):
+        edge_copy(k, 1 - side).wait_recv()
 
     for k in range(ITERS):
         last = k == ITERS - 1
@@ -627,34 +642,46 @@
                             near[side, pl.ds(m, 1)] = field[1, m, pl.ds(around + rims[side], 1)]
                         near_copy(side).start()
 
-                @pl.when(~is_stator_face)
+            def begin(far, close):
+                if k == 0:
+
+                    @pl.when(~is_stator_face)
+                    def _():
+                        coef_copy(far).start()
+                        send_part(0, far)
+
+                else:
+                    send_part(k, far)
+                arrive(k, close)
+                fix_side(k, close, received)
+                if k == 0:
+                    take_edges(1, (close,))
+                    edge_copy(1, close).start()
+                else:
+                    send_part(k, close)
+
+                @pl.when(is_stator_face)
                 def _():
-                    send_parts(0)
-                    for side in range(2):
-                        coef_copy(side).start()
-
-            else:
-                send_parts(k)
+                    relay(k)
+
+                arrive(k, far)
+                fix_side(k, far, received)
+                if k == 0:
+
+                    @pl.when(is_stator_face)
+                    def _():
+                        take_edges(1, (far,))
+                        edge_copy(1, far).start()
+
+            by_place(begin)
 
             @pl.when(is_stator_face)
             def _():
-                relay(k)
-
-            both_edges(k).wait_recv()
-            fix_sides(k, received)
-
-            @pl.when(is_stator_face)
-            def _():
-                if k == 0:
-                    take_edges(1)
-                    for side in range(2):
-                        edge_copy(1, side).start()
                 if k == 0:
                     relay_cross()
                 relay(k + 1)
                 if k == 0:
-                    for side in range(2):
-                        coef_copy(side).start()
+                    by_place(lambda far, close: coef_copy(far).start())
                     both_near().wait_recv()
                 wait_forward(k)
                 fix_layer(k, 0, facing_of(k, None))
@@ -676,15 +703,20 @@
                 wait_forward(k)
                 fix_layer(k, 0, facing_of(k, extra))
                 rim_copy(k + 1, 1).start()
-                both_edges(1).wait_recv()
-                fix_sides(k, received, 1)
+                for side in range(2):
+                    arrive(1, side)
+                    fix_side(k, side, received, 1)
 
             @pl.when(~is_stator_face)
             def _():
-                both_parts(0).wait_recv()
-                for side in range(2):
-                    coef_copy(side).wait_recv()
-                fix_sides(k, completed)
+                def finish(far, close):
+                    arrive(1, close)
+                    fix_side(k, close, received)
+                    part_copy(0, 1 - far).wait_recv()
+                    coef_copy(1 - far).wait_recv()
+                    fix_side(k, far, completed)
+
+                by_place(finish)
 
                 @pl.when(block < blocks - 1)
                 def _():
@@ -703,18 +735,25 @@
                 rim_copy(k + 1, 0).start()
 
             take_edges(k + 1)
-            for side in range(2):
-                edge_copy(k + 1, side).start()
+
+            def exchange(far, close):
+                edge_copy(k + 1, far).start()
+                edge_copy(k + 1, close).start()
+
+            by_place(exchange)
         else:
-            both_parts(k).wait_recv()
+            both_parts(2).wait_recv()
 
             @pl.when(is_stator_face)
             def _():
-                for side in range(2):
-                    coef_copy(side).wait_recv()
-                complete_parts(k - 1)
-
-            fix_sides(k, completed)
+                coef_copy(0).wait_recv()
+                complete_parts(2)
+
+            def end(far, close):
+                fix_side(k, close, sent)
+                fix_side(k, far, completed)
+
+            by_place(end)
             wait_sends()
 
             @pl.when(block < blocks - 1)
@@ -786,11 +825,11 @@
                 dma((7,)),
                 pltpu.SemaphoreType.REGULAR,
                 dma((3,)),
-                dma((3,)),
+                dma((3, 2)),
                 dma((2,)),
                 dma((2,)),
-                dma((2,)),
-                dma((2,)),
+                dma,
+                dma,
                 dma,
                 dma,
                 dma((ITERS, min(blocks - 1, 2))),

time: 24.6 us -> 23.9 us (0.972)
  Pallas kernels: 22.4 us -> 21.6 us
    pallas_call x1, Pallas kernels: 22.4 us -> 21.6 us  [sweeps(): pl.pallas_call(functools.partial(kernel, sectors, blocks, layers, around)...]
where the time goes in v4:
time: 23.9 us; the launch traced here: 23.7 us
  Pallas kernels  21.6 us (90%)
  between operations  1.29 us (5%)
  other arithmetic  0.75 us (3%)
    pallas_call x1, Pallas kernels, sweeps(): pl.pallas_call(functools.partial(kernel, sectors, blocks, layers, around)...  21.6 us
    sub x1, other arithmetic, sweeps(): return (0.0 - negative, 0.0 - negative - previous)  0.75 us

profile of v4, /device:TPU:1, one launch (start us, length us, event | category | flops | bytes accessed | tf_op | source)
XLA Modules:
  0.0 23.7 jit_solution(2332777508635737339)
XLA Ops:
  1.3 21.6 %shard_map.86 = (f32[5,64,128]{2,1,0:T(8,128)S(1)}, f32[5,64,128]{2,1,0:T(8,128)S(1)}) custom-call(f32[5,64,128]{2,1,0:T(8,128)} %bitcast.7, f32[5,64,128]{2,1,0:T(8,128)} %bitcast.8, bf16[3,5,5,8,8,128]{5,4,3,2,1,0:T(8,128)(2,1)} %face_ref.1, bf16[5,5,8,8,128]{4,3,2,1,0:T(8,128)(2,1)} %inverse_ref.1, s32[1]{0:T(128)S(6)} %copy.9.offset_hbm, s32[8]{0:T(128)} %cells_hbm.1, ...), custom_call_target="tpu_custom_call" | custom-call | tf_op jit(solution)/shard_map/pallas_call | solution.py:789
  22.9 0.7 %bitcast_subtract_fusion = (f32[5,8,8,128]{3,2,1,0:T(8,128)}, f32[5,8,8,128]{3,2,1,0:T(8,128)}) fusion(f32[5,64,128]{2,1,0:T(8,128)S(1)} %get-tuple-element.5, f32[5,64,128]{2,1,0:T(8,128)S(1)} %get-tuple-element.4), kind=kLoop, calls=%fused_computation | loop fusion | flops 81920 | bytes 655360 | tf_op jit(solution)/shard_map/sub | solution.py:849

commit v5 on v4

--- a/solution.py
+++ b/solution.py
@@ -122,11 +122,6 @@
     def _():
         greet(sector, block + 1)
 
-    @pl.when(is_rotor_face)
-    def _():
-        for step in range(highs):
-            greet(((high + step) % highs) * lows + low, first)
-
     @pl.when(is_stator_face)
     def _():
         for step in range(highs):
@@ -155,7 +150,7 @@
         copy.start()
 
     greetings = 2 - is_start.astype(jnp.int32) + (block > 0).astype(jnp.int32) + (block < blocks - 1).astype(jnp.int32)
-    greetings += jnp.where(is_rotor_face, highs, 0) + jnp.where(is_stator_face, highs + lows - 1, 0)
+    greetings += jnp.where(is_rotor_face, highs, 0) + jnp.where(is_stator_face, lows - 1, 0)
 
     @pl.when(is_end)
     def _():
@@ -231,20 +226,29 @@
         return remote(
             field.at[k, :, plane(1 if side else layers)],
             rim_in.at[k, side],
-            rim_send.at[k, 1 - side],
+            rim_send.at[1 - side],
             rim_recv.at[k, 1 - side],
             (sector, block - 1 if side else block + 1),
         )
 
+    def sent_rims(side):
+        ours = rim_in.at[:, side]
+        to = (sector, block - 1 if side else block + 1)
+        return remote(ours, ours, rim_send.at[1 - side], rim_recv.at[0, 1 - side], to)
+
     def row_source(k):
         return row_out.at[k // 2] if k % 2 else field.at[k, :, plane(layers)]
 
     def row_copy(k, step):
         to = (high + step) % highs
-        return remote(row_source(k), rows[k].at[high], row_send.at[k], row_recv.at[k], (to * lows + low, first))
+        return remote(row_source(k), rows[k].at[high], row_send, row_recv.at[k], (to * lows + low, first))
 
     def all_rows(k):
-        return remote(rows[k], rows[k], row_send.at[k], row_recv.at[k], (sector, first))
+        return remote(rows[k], rows[k], row_send, row_recv.at[k], (sector, first))
+
+    def sent_rows():
+        part = forward.at[:, pl.ds(0, highs)]
+        return remote(part, part, row_send, row_recv.at[0], (sector, first))
 
     def cross_copy(step):
         to = (high + step) % highs
@@ -255,11 +259,15 @@
 
     def forward_copy(k, step):
         to = (high * lows + partner(step), first)
-        return remote(forward.at[k, step], picked[k].at[low], forward_send.at[k], forward_recv.at[k], to)
+        return remote(forward.at[k, step], picked[k].at[low], forward_send, forward_recv.at[k], to)
 
     def all_forwards(k):
         part = forward.at[k, pl.ds(1, lows - 1)]
-        return remote(part, part, forward_send.at[k], forward_recv.at[k], (sector, first))
+        return remote(part, part, forward_send, forward_recv.at[k], (sector, first))
+
+    def sent_forwards():
+        part = forward.at[:, pl.ds(1, lows - 1)]
+        return remote(part, part, forward_send, forward_recv.at[0], (sector, first))
 
     def cross_forward_copy(step):
         to = (high * lows + partner(step), first)
@@ -571,29 +579,25 @@
         both_edges(0).wait_send()
         both_edges(2).wait_send()
         both_parts(2).wait_send()
-        for k in range(ITERS):
-
-            @pl.when(block > 0)
-            def _():
-                rim_copy(k, 1).wait_send()
-
-            @pl.when(has_upper)
-            def _():
-                rim_copy(k, 0).wait_send()
+        @pl.when(block > 0)
+        def _():
+            sent_rims(1).wait_send()
+
+        @pl.when(has_upper)
+        def _():
+            sent_rims(0).wait_send()
 
         @pl.when(is_rotor_face)
         def _():
             all_crosses().wait_send()
-            for k in range(ITERS):
-                all_rows(k).wait_send()
+            sent_rows().wait_send()
 
         @pl.when(is_stator_face)
         def _():
             both_near().wait_send()
             both_edges(1).wait_send()
             all_cross_forwards().wait_send()
-            for k in range(ITERS):
-                all_forwards(k).wait_send()
+            sent_forwards().wait_send()
 
         @pl.when(~is_stator_face)
         def _():
@@ -832,11 +836,11 @@
                 dma,
                 dma,
                 dma,
+                dma((min(blocks - 1, 2),)),
                 dma((ITERS, min(blocks - 1, 2))),
-                dma((ITERS, min(blocks - 1, 2))),
+                dma,
                 dma((ITERS,)),
-                dma((ITERS,)),
-                dma((ITERS,)),
+                dma,
                 dma((ITERS,)),
                 dma,
                 dma,

time: 23.9 us -> 23.8 us (level)
  no operation moved by 1% of the time
where the time goes in v5:
time: 23.8 us; the launch traced here: 23.5 us
  Pallas kernels  21.5 us (90%)
  between operations  1.29 us (5%)
  other arithmetic  0.75 us (3%)
    pallas_call x1, Pallas kernels, sweeps(): pl.pallas_call(functools.partial(kernel, sectors, blocks, layers, around)...  21.5 us
    sub x1, other arithmetic, sweeps(): return (0.0 - negative, 0.0 - negative - previous)  0.75 us

profile of v5, /device:TPU:1, one launch (start us, length us, event | category | flops | bytes accessed | tf_op | source)
XLA Modules:
  0.0 23.5 jit_solution(17890586586180714919)
XLA Ops:
  1.3 21.5 %shard_map.86 = (f32[5,64,128]{2,1,0:T(8,128)S(1)}, f32[5,64,128]{2,1,0:T(8,128)S(1)}) custom-call(f32[5,64,128]{2,1,0:T(8,128)} %bitcast.7, f32[5,64,128]{2,1,0:T(8,128)} %bitcast.8, bf16[3,5,5,8,8,128]{5,4,3,2,1,0:T(8,128)(2,1)} %face_ref.1, bf16[5,5,8,8,128]{4,3,2,1,0:T(8,128)(2,1)} %inverse_ref.1, s32[1]{0:T(128)S(6)} %copy.9.offset_hbm, s32[8]{0:T(128)} %cells_hbm.1, ...), custom_call_target="tpu_custom_call" | custom-call | tf_op jit(solution)/shard_map/pallas_call | solution.py:793
  22.8 0.7 %bitcast_subtract_fusion = (f32[5,8,8,128]{3,2,1,0:T(8,128)}, f32[5,8,8,128]{3,2,1,0:T(8,128)}) fusion(f32[5,64,128]{2,1,0:T(8,128)S(1)} %get-tuple-element.5, f32[5,64,128]{2,1,0:T(8,128)S(1)} %get-tuple-element.4), kind=kLoop, calls=%fused_computation | loop fusion | flops 81920 | bytes 655360 | tf_op jit(solution)/shard_map/sub | solution.py:853

commit v6 on v5

--- a/solution.py
+++ b/solution.py
@@ -219,6 +219,11 @@
     def coef_copy(side):
         return remote(coef.at[side], coef_in.at[side], coef_send, coef_recv, beside(side))
 
+    def coef_pieces(side, pieces):
+        for n in pieces:
+            piece = pl.ds(n * comps * layers, comps * layers)
+            remote(coef.at[side, piece], coef_in.at[side, piece], coef_send, coef_recv, beside(side)).start()
+
     def near_copy(side):
         return remote(near.at[side], near_in.at[side], near_send, near_recv, beside(side))
 
@@ -651,7 +656,7 @@
 
                     @pl.when(~is_stator_face)
                     def _():
-                        coef_copy(far).start()
+                        coef_pieces(far, range(comps))
                         send_part(0, far)
 
                 else:
@@ -685,10 +690,12 @@
                     relay_cross()
                 relay(k + 1)
                 if k == 0:
-                    by_place(lambda far, close: coef_copy(far).start())
+                    by_place(lambda far, close: coef_pieces(far, range(0, 2)))
                     both_near().wait_recv()
                 wait_forward(k)
                 fix_layer(k, 0, facing_of(k, None))
+                if k == 0:
+                    by_place(lambda far, close: coef_pieces(far, range(2, 4)))
 
             send_rims(k + 1)
         elif not last:
@@ -743,6 +750,10 @@
             def exchange(far, close):
                 edge_copy(k + 1, far).start()
                 edge_copy(k + 1, close).start()
+
+                @pl.when(is_stator_face)
+                def _():
+                    coef_pieces(far, range(4, comps))
 
             by_place(exchange)
         else:

time: 23.8 us -> 23.6 us (level)
  no operation moved by 1% of the time
where the time goes in v6:
time: 23.6 us; the launch traced here: 23.3 us
  Pallas kernels  21.3 us (90%)
  between operations  1.29 us (5%)
  other arithmetic  0.75 us (3%)
    pallas_call x1, Pallas kernels, sweeps(): pl.pallas_call(functools.partial(kernel, sectors, blocks, layers, around)...  21.3 us
    sub x1, other arithmetic, sweeps(): return (0.0 - negative, 0.0 - negative - previous)  0.75 us

profile of v6, /device:TPU:1, one launch (start us, length us, event | category | flops | bytes accessed | tf_op | source)
XLA Modules:
  0.0 23.3 jit_solution(2456124391801819883)
XLA Ops:
  1.3 21.3 %shard_map.86 = (f32[5,64,128]{2,1,0:T(8,128)S(1)}, f32[5,64,128]{2,1,0:T(8,128)S(1)}) custom-call(f32[5,64,128]{2,1,0:T(8,128)} %bitcast.7, f32[5,64,128]{2,1,0:T(8,128)} %bitcast.8, bf16[3,5,5,8,8,128]{5,4,3,2,1,0:T(8,128)(2,1)} %face_ref.1, bf16[5,5,8,8,128]{4,3,2,1,0:T(8,128)(2,1)} %inverse_ref.1, s32[1]{0:T(128)S(6)} %copy.9.offset_hbm, s32[8]{0:T(128)} %cells_hbm.1, ...), custom_call_target="tpu_custom_call" | custom-call | tf_op jit(solution)/shard_map/pallas_call | solution.py:804
  22.6 0.7 %bitcast_subtract_fusion = (f32[5,8,8,128]{3,2,1,0:T(8,128)}, f32[5,8,8,128]{3,2,1,0:T(8,128)}) fusion(f32[5,64,128]{2,1,0:T(8,128)S(1)} %get-tuple-element.5, f32[5,64,128]{2,1,0:T(8,128)S(1)} %get-tuple-element.4), kind=kLoop, calls=%fused_computation | loop fusion | flops 81920 | bytes 655360 | tf_op jit(solution)/shard_map/sub | solution.py:864

commit v7 on v6

--- a/solution.py
+++ b/solution.py
@@ -656,8 +656,8 @@
 
                     @pl.when(~is_stator_face)
                     def _():
+                        send_part(0, far)
                         coef_pieces(far, range(comps))
-                        send_part(0, far)
 
                 else:
                     send_part(k, far)

time: 23.6 us -> 23.6 us (level)
  no operation moved by 1% of the time
where the time goes in v7:
time: 23.6 us; the launch traced here: 23.3 us
  Pallas kernels  21.3 us (90%)
  between operations  1.29 us (5%)
  other arithmetic  0.75 us (3%)
    pallas_call x1, Pallas kernels, sweeps(): pl.pallas_call(functools.partial(kernel, sectors, blocks, layers, around)...  21.3 us
    sub x1, other arithmetic, sweeps(): return (0.0 - negative, 0.0 - negative - previous)  0.75 us

profile of v7, /device:TPU:1, one launch (start us, length us, event | category | flops | bytes accessed | tf_op | source)
XLA Modules:
  0.0 23.3 jit_solution(2738532988480309627)
XLA Ops:
  1.3 21.3 %shard_map.86 = (f32[5,64,128]{2,1,0:T(8,128)S(1)}, f32[5,64,128]{2,1,0:T(8,128)S(1)}) custom-call(f32[5,64,128]{2,1,0:T(8,128)} %bitcast.7, f32[5,64,128]{2,1,0:T(8,128)} %bitcast.8, bf16[3,5,5,8,8,128]{5,4,3,2,1,0:T(8,128)(2,1)} %face_ref.1, bf16[5,5,8,8,128]{4,3,2,1,0:T(8,128)(2,1)} %inverse_ref.1, s32[1]{0:T(128)S(6)} %copy.9.offset_hbm, s32[8]{0:T(128)} %cells_hbm.1, ...), custom_call_target="tpu_custom_call" | custom-call | tf_op jit(solution)/shard_map/pallas_call | solution.py:804
  22.6 0.7 %bitcast_subtract_fusion = (f32[5,8,8,128]{3,2,1,0:T(8,128)}, f32[5,8,8,128]{3,2,1,0:T(8,128)}) fusion(f32[5,64,128]{2,1,0:T(8,128)S(1)} %get-tuple-element.5, f32[5,64,128]{2,1,0:T(8,128)S(1)} %get-tuple-element.4), kind=kLoop, calls=%fused_computation | loop fusion | flops 81920 | bytes 655360 | tf_op jit(solution)/shard_map/sub | solution.py:864
